TPU v7x, 512 devices: a 4x2x32 block of a 4x16x32 slice. The times are simulated.
512 devices in a mesh: parts: 2 (over y), row: 32 (over z), col: 4 (over x), sub: 2 (over core).
Axes of the slice: x: 4, y: 2, z: 32, core: 2. Of those that a mesh axis runs over, the one named last changes fastest.
The devices are a block of a 4x16x32 slice.
Arguments:
- pair: float32 [768, 384, 128], P(('parts', 'row'), ('col', 'sub')), parts along dimension 0, may hold values from -250 to 250, as said below
- residue_mask: int32 [768], P('parts'), parts along dimension 0, may hold values from 0 to 1, as said below
- tri_norm_gain: float32 [128], replicated, may hold values from 0.25 to 1.75
- tri_in_weight: bfloat16 [128, 4, 128], replicated, may hold values from -0.5 to 0.5
- tri_gate_weight: bfloat16 [128, 128], replicated, may hold values from -0.5 to 0.5
- tri_out_norm_gain: float32 [128], replicated, may hold values from 0.25 to 1.75
- tri_out_weight: bfloat16 [128, 128], replicated, may hold values from -0.5 to 0.5
- att_norm_gain: float32 [128], replicated, may hold values from 0.25 to 1.75
- att_proj_weight: bfloat16 [128, 4, 128], replicated, may hold values from -0.5 to 0.5
- att_bias_weight: bfloat16 [128, 4], replicated, may hold values from -15 to 15
- att_out_weight: bfloat16 [128, 128], replicated, may hold values from -0.5 to 0.5
Outputs:
- pair_out: float32 [768, 384, 128], P(('parts', 'row'), ('col', 'sub')), parts along dimension 0
There are 2 independent parts, one for each index of `parts`. A program takes and returns all parts, laid end to end along the dimension named above; an argument that names none is the same for every part. Nothing has to cross between parts.
Inputs may be any that keep to these rules, and one draw needn't show every extreme that they name: The pair entries are finite. `residue_mask`: 0 on every residue at or above a length of at least 192 and less than 384; below it 1, except some unresolved residues that are 0; residue 0 is always 1.
All inputs are finite; a program needn't handle non-finite values.
Results may differ from a plain program's by a relative error of at most 0.0032.
Values may be sent and summed in bfloat16 or wider, within the bound.
A program may use at most 64 MiB of HBM per device.

v0:
```python
import math

import jax
import jax.numpy as jnp
from jax import lax
from jax.sharding import PartitionSpec as P

epsilon = 1e-05
mask_penalty = 1000000000.0


def split_up(array, dim, devices):
    lengths = array.shape
    pieces = array.reshape(*lengths[:dim], devices, lengths[dim] // devices, *lengths[dim + 1 :])
    return jnp.moveaxis(pieces, dim, 0)


def sum_at_owner(array, axis, dim):
    devices = lax.axis_size(axis)
    pieces = lax.all_to_all(split_up(array, dim, devices), axis, 0, 0, tiled=True)
    return jnp.sum(pieces, axis=0)


def in_one_piece(arrays, axis, dim, along):
    widths = [a.shape[along] for a in arrays]
    both = jnp.concatenate(arrays, axis=along)
    result = lax.all_gather(both, axis, axis=dim, tiled=True)
    return tuple(jnp.split(result, [sum(widths[:k]) for k in range(1, len(widths))], axis=along))


def from_everyone(array, axis):
    copies = jnp.broadcast_to(array, (lax.axis_size(axis), *array.shape))
    return lax.all_to_all(copies, axis, split_axis=0, concat_axis=0, tiled=True)


def laid_out(pieces, dim):
    lengths = list(pieces.shape[1:])
    lengths[dim] *= pieces.shape[0]
    return jnp.moveaxis(pieces, 0, dim).reshape(lengths)


def gathered_copies(array, axis, dim):
    pieces = from_everyone(array, axis)
    return laid_out(pieces, dim)


def norm_last(values_in, gain):
    center = jnp.mean(values_in, axis=-1, keepdims=True)
    centered = values_in - center
    variance = jnp.mean(centered * centered, axis=-1, keepdims=True)
    return centered * lax.rsqrt(variance + epsilon) * gain


def project(normed, weight):
    flat_rows = normed.reshape(-1, normed.shape[-1])
    product = jnp.dot(flat_rows, weight, preferred_element_type=jnp.float32)
    return product.reshape(normed.shape[:-1] + (weight.shape[1],))


def body(
    pair,
    residue_mask,
    tri_norm_gain,
    tri_in_weight,
    tri_gate_weight,
    tri_out_norm_gain,
    tri_out_weight,
    att_norm_gain,
    att_proj_weight,
    att_bias_weight,
    att_out_weight,
):
    rows_here, cols_here, chan_here = pair.shape
    residues = cols_here * lax.axis_size(("col", "sub"))
    row_offset = lax.axis_index("row") * rows_here
    col_offset = lax.axis_index(("col", "sub")) * cols_here
    residue_live = residue_mask.astype(jnp.float32)
    live_rows = lax.dynamic_slice_in_dim(residue_live, row_offset, rows_here)
    live_cols = lax.dynamic_slice_in_dim(residue_live, col_offset, cols_here)
    pair_live = (live_rows[:, None] * live_cols[None, :])[:, :, None]
    tri_normed = norm_last(pair, tri_norm_gain).astype(jnp.bfloat16)
    in_width = tri_in_weight.shape[2]
    projected = project(tri_normed, tri_in_weight.reshape(tri_in_weight.shape[0], -1)).reshape(
        rows_here, cols_here, 4, in_width
    )
    left_factor = (jax.nn.sigmoid(projected[:, :, 0]) * projected[:, :, 1] * pair_live).astype(
        jnp.bfloat16
    )
    right_factor = (jax.nn.sigmoid(projected[:, :, 2]) * projected[:, :, 3] * pair_live).astype(
        jnp.bfloat16
    )
    terms = jnp.einsum(
        "ikh,jkh->ijh",
        left_factor,
        lax.all_gather(right_factor, "row", axis=0, tiled=True),
        preferred_element_type=jnp.float32,
    )
    tri_sum = sum_at_owner(terms, ("col", "sub"), 1)
    hidden_normed = norm_last(tri_sum, tri_out_norm_gain).astype(jnp.bfloat16)
    tri_gate = jax.nn.sigmoid(project(tri_normed, tri_gate_weight))
    pair_mid = pair + tri_gate * project(hidden_normed, tri_out_weight)
    att_normed = norm_last(pair_mid, att_norm_gain).astype(jnp.bfloat16)
    head_width = att_proj_weight.shape[2]
    heads_here = att_bias_weight.shape[1]
    head_size = head_width // heads_here
    projected = project(att_normed, att_proj_weight.reshape(att_proj_weight.shape[0], -1)).reshape(
        rows_here, cols_here, 4, head_width
    )
    queries = (projected[:, :, 0] * head_size ** (-0.5)).astype(jnp.bfloat16)
    key_rows = projected[:, :, 1].astype(jnp.bfloat16)
    value_rows = projected[:, :, 2].astype(jnp.bfloat16)
    att_gate = jax.nn.sigmoid(projected[:, :, 3])
    pair_bias = project(att_normed, att_bias_weight).astype(jnp.bfloat16)
    key_all, value_all = in_one_piece((key_rows, value_rows), ("col", "sub"), 1, 0)
    bias_all_rows = gathered_copies(pair_bias, "row", 0)
    bias_panel = lax.all_to_all(
        bias_all_rows, ("col", "sub"), split_axis=0, concat_axis=1, tiled=True
    )
    mask_row = (residue_live - 1.0) * mask_penalty
    head_bias = jnp.transpose(bias_panel.astype(jnp.float32), (2, 0, 1)) + mask_row[None, None, :]
    block_rows = math.gcd(rows_here, max(1, 512 // cols_here))
    blocks = rows_here // block_rows

    def attend(block_items):
        query_block, key_block, value_block = block_items
        scores = (
            jnp.einsum(
                "ijhd,ikhd->ihjk", query_block, key_block, preferred_element_type=jnp.float32
            )
            + head_bias[None]
        )
        row_max = jnp.max(scores, axis=-1, keepdims=True)
        raised = jnp.exp(scores - row_max)
        weights = (raised / jnp.sum(raised, axis=-1, keepdims=True)).astype(jnp.bfloat16)
        return jnp.einsum(
            "ihjk,ikhd->ijhd", weights, value_block, preferred_element_type=jnp.float32
        )

    attended = lax.map(
        attend,
        (
            queries.reshape(blocks, block_rows, cols_here, heads_here, head_size),
            key_all.reshape(blocks, block_rows, residues, heads_here, head_size),
            value_all.reshape(blocks, block_rows, residues, heads_here, head_size),
        ),
    )
    gated = (attended.reshape(rows_here, cols_here, head_width) * att_gate).astype(jnp.bfloat16)
    return pair_mid + project(gated, att_out_weight)


def solution(mesh):
    placed = (
        P(("parts", "row"), ("col", "sub"), None),
        P("parts"),
        P(),
        P(),
        P(),
        P(),
        P(),
        P(),
        P(),
        P(),
        P(),
    )
    return jax.shard_map(
        body,
        mesh=mesh,
        in_specs=placed,
        out_specs=P(("parts", "row"), ("col", "sub"), None),
        check_vma=False,
    )
```

profile of v0, /device:TPU:33, one launch (start us, length us, event | category | flops | bytes accessed | tf_op | source)
XLA Modules:
  0.0 341.0 jit_solution(17317028375399813214)
XLA Ops:
  8.6 1.2 multiply_reduce_fusion.2
  13.5 147.5 %all-gather.3.cloned.1.call-done = bf16[384,48,128]{2,1,0:T(8,128)(2,1)} async-done(((bf16[12,48,128]{2,1,0:T(8,128)(2,1)}), bf16[384,48,128]{2,1,0:T(8,128)(2,1)}) %all-gather.3.cloned.1.call-update) | async-done | bytes 4718608 | tf_op jit(solution)/shard_map/all_gather | solution.py:95
  160.9 17.8 %copy.101 = bf16[384,48,128]{1,0,2:T(8,128)(2,1)} copy(bf16[384,48,128]{2,1,0:T(8,128)(2,1)} %all-gather.3.cloned.1.call-done) | data formatting | bytes 9437184 | tf_op jit(solution)/shard_map/all_gather | solution.py:95
  178.7 9.1 %convolution_bitcast_fusion.1 = f32[12,384,128]{1,0,2:T(8,128)S(1)} fusion(bf16[384,48,128]{1,0,2:T(8,128)(2,1)} %copy.101, bf16[12,48,128]{1,0,2:T(8,128)(2,1)} %copy.102), kind=kOutput, calls=%fused_computation.18 | convolution fusion | flops 56623104 | bytes 7225344 | tf_op jit(solution)/shard_map/ikh,jkh->ijh/dot_general | solution.py:92
  187.8 2.1 copy.103
  190.0 3.3 copy.104
  193.2 23.9 %all-to-all-start = ((f32[8,12,48,128]{3,2,1,0:T(8,128)}), f32[8,12,48,128]{3,2,1,0:T(8,128)S(1)}, u32[]{:S(2)}, u32[]{:S(2)}) async-start(f32[8,12,48,128]{3,2,1,0:T(8,128)} %copy.104), calls=%async_computation | async-start | bytes 4718592 | tf_op jit(solution)/shard_map/all_to_all | solution.py:20
  217.7 28.5 %all-to-all-done = f32[8,12,48,128]{3,2,1,0:T(8,128)S(1)} async-done(((f32[8,12,48,128]{3,2,1,0:T(8,128)}), f32[8,12,48,128]{3,2,1,0:T(8,128)S(1)}, u32[]{:S(2)}, u32[]{:S(2)}) %all-to-all-start) | async-done | bytes 2359328 | tf_op jit(solution)/shard_map/all_to_all | solution.py:20
  250.4 12.5 %all-to-all-start.1 = ((bf16[32,2,1152]{2,1,0:T(2,128)(2,1)}), bf16[32,2,1152]{2,1,0:T(2,128)(2,1)S(1)}, u32[]{:S(2)}, u32[]{:S(2)}) async-start(bf16[32,2,1152]{2,1,0:T(2,128)(2,1)} %reshape.185), calls=%async_computation.1 | async-start | bytes 294912 | tf_op jit(solution)/shard_map/all_to_all | solution.py:33
  263.0 30.6 %all-to-all-done.1 = bf16[32,2,1152]{2,1,0:T(2,128)(2,1)S(1)} async-done(((bf16[32,2,1152]{2,1,0:T(2,128)(2,1)}), bf16[32,2,1152]{2,1,0:T(2,128)(2,1)S(1)}, u32[]{:S(2)}, u32[]{:S(2)}) %all-to-all-start.1) | async-done | bytes 147488 | tf_op jit(solution)/shard_map/all_to_all | solution.py:33
  293.9 1.2 reshape.187
  295.1 5.9 %all-to-all-start.2 = ((bf16[8,2,4608]{2,1,0:T(2,128)(2,1)}), bf16[8,2,4608]{2,1,0:T(2,128)(2,1)S(1)}, u32[]{:S(2)}, u32[]{:S(2)}) async-start(bf16[8,2,4608]{2,1,0:T(2,128)(2,1)} %reshape.187), calls=%async_computation.2 | async-start | bytes 294912 | tf_op jit(solution)/shard_map/all_to_all | solution.py:116
  301.3 5.2 %all-to-all-done.2 = bf16[8,2,4608]{2,1,0:T(2,128)(2,1)S(1)} async-done(((bf16[8,2,4608]{2,1,0:T(2,128)(2,1)}), bf16[8,2,4608]{2,1,0:T(2,128)(2,1)S(1)}, u32[]{:S(2)}, u32[]{:S(2)}) %all-to-all-start.2) | async-done | bytes 147488 | tf_op jit(solution)/shard_map/all_to_all | solution.py:116
  308.1 1.8 fusion.68
  309.9 1.4 copy.107
  312.1 18.8 %while.10 = (s32[]{:T(128)}, f32[6,2,48,4,32]{2,4,3,1,0:T(8,128)}, bf16[6,2,384,4,32]{2,4,3,1,0:T(8,128)(2,1)}, bf16[6,2,48,4,32]{2,4,3,1,0:T(8,128)(2,1)S(1)}, ...) while((s32[]{:T(128)}, f32[6,2,48,4,32]{2,4,3,1,0:T(8,128)}, ...), condition=%wide.region_10.11_spmd, body=%wide.region_7.10_spmd.sunk | while | flops 29344896 | bytes 3220045 | solution.py:139
  312.8 2.4 fusion.91
  316.0 2.4 fusion.91
  319.1 2.4 fusion.91
  322.2 2.4 fusion.91
  325.4 2.4 fusion.91
  328.5 2.4 fusion.91
  330.9 1.4 copy.113
  332.3 1.9 convolution_add_fusion.1
  (80 shorter events, 17.6 us)
Async XLA Ops:
  6.5 240.2 %copy-start = (bf16[128,128]{1,0:T(8,128)(2,1)S(1)}, bf16[128,128]{1,0:T(8,128)(2,1)}, u32[]{:S(2)}) copy-start(bf16[128,128]{1,0:T(8,128)(2,1)} %param.19) | copy-start | bytes 98308
  6.6 4.4 %copy-start.1 = (f32[12,48,128]{2,1,0:T(8,128)S(1)}, f32[12,48,128]{2,1,0:T(8,128)}, u32[]{:S(2)}) copy-start(f32[12,48,128]{2,1,0:T(8,128)} %param.13) | copy-start | bytes 884740
  6.6 4.4 %copy-start.7 = (f32[128]{0:T(128)S(1)}, f32[128]{0:T(128)}, u32[]{:S(2)}) copy-start(f32[128]{0:T(128)} %param.15) | copy-start | bytes 1540
  6.6 154.4 %all-gather.3.cloned.1.call-start = ((), (), s32[]{:S(2)}) async-start(), calls=%async_computation.3 | async-start | bytes 4866048 | tf_op jit(solution)/shard_map/all_gather | solution.py:95
  193.2 24.0 %copy-start.3 = (bf16[128,4,128]{2,1,0:T(4,128)(2,1)S(1)}, bf16[128,4,128]{2,1,0:T(4,128)(2,1)}, u32[]{:S(2)}) copy-start(bf16[128,4,128]{2,1,0:T(4,128)(2,1)} %param.21) | copy-start | bytes 393220
  193.2 24.1 %copy-start.9 = (bf16[128,128]{1,0:T(8,128)(2,1)S(1)}, bf16[128,128]{1,0:T(8,128)(2,1)}, u32[]{:S(2)}) copy-start(bf16[128,128]{1,0:T(8,128)(2,1)} %param.17) | copy-start | bytes 98308
  193.2 53.0 %all-to-all-start = ((f32[8,12,48,128]{3,2,1,0:T(8,128)}), f32[8,12,48,128]{3,2,1,0:T(8,128)S(1)}, u32[]{:S(2)}, u32[]{:S(2)}) async-start(f32[8,12,48,128]{3,2,1,0:T(8,128)} %copy.104), calls=%async_computation | async-start | bytes 4718592 | tf_op jit(solution)/shard_map/all_to_all | solution.py:20
  217.2 90.9 %all-gather.5.cloned.1.call-start = ((), (), s32[]{:S(2)}) async-start(), calls=%async_computation.4 | async-start | bytes 2654208 | tf_op jit(solution)/shard_map/all_gather | solution.py:27
  217.7 29.0 %copy-start.8 = (f32[128]{0:T(128)S(1)}, f32[128]{0:T(128)}, u32[]{:S(2)}) copy-start(f32[128]{0:T(128)} %param.18) | copy-start | bytes 1540
  246.4 1.1 copy-start.5
  247.9 53.2 %copy-start.2 = (f32[12,48,4,128]{3,1,2,0:T(8,128)}, f32[12,48,4,128]{3,1,2,0:T(8,128)S(1)}, u32[]{:S(2)}) copy-start(f32[12,48,4,128]{3,1,2,0:T(8,128)S(1)} %get-tuple-element.67) | copy-start | bytes 3538948
  247.9 0.9 copy-start.6
  247.9 15.0 %copy-start.4 = (s32[384]{0:T(512)S(1)}, s32[384]{0:T(512)}, u32[]{:S(2)}) copy-start(s32[384]{0:T(512)} %param.14) | copy-start | bytes 4612
  250.4 43.1 %all-to-all-start.1 = ((bf16[32,2,1152]{2,1,0:T(2,128)(2,1)}), bf16[32,2,1152]{2,1,0:T(2,128)(2,1)S(1)}, u32[]{:S(2)}, u32[]{:S(2)}) async-start(bf16[32,2,1152]{2,1,0:T(2,128)(2,1)} %reshape.185), calls=%async_computation.1 | async-start | bytes 294912 | tf_op jit(solution)/shard_map/all_to_all | solution.py:33
  295.1 11.4 %all-to-all-start.2 = ((bf16[8,2,4608]{2,1,0:T(2,128)(2,1)}), bf16[8,2,4608]{2,1,0:T(2,128)(2,1)S(1)}, u32[]{:S(2)}, u32[]{:S(2)}) async-start(bf16[8,2,4608]{2,1,0:T(2,128)(2,1)} %reshape.187), calls=%async_computation.2 | async-start | bytes 294912 | tf_op jit(solution)/shard_map/all_to_all | solution.py:116
  312.0 20.2 %copy-start.10 = (bf16[128,128]{1,0:T(8,128)(2,1)S(1)}, bf16[128,128]{1,0:T(8,128)(2,1)}, u32[]{:S(2)}) copy-start(bf16[128,128]{1,0:T(8,128)(2,1)} %param.23) | copy-start | bytes 98308
Sparse Core Ops, SparseCore 0:
  12.4 148.5 all-gather.2
  248.9 31.5 all-gather.4
where the time goes:
time: 342 us; the launch traced here: 341 us
  waiting for transfers between devices  212 us (62%)
  starting transfers between devices  42.3 us (12%)
  local copies, waits for them, and re-layouts  35.8 us (10%)
  matrix products  31.6 us (9%)
  between operations  13.8 us (4%)
  other arithmetic  5.57 us (2%)
    all_gather x1, waiting for transfers between devices, body(): lax.all_gather(right_factor, 'row', axis=0, tiled=True)  147 us
    all_to_all x1, waiting for transfers between devices, from_everyone(): return lax.all_to_all(copies, axis, split_axis=0, concat_axis=0, tiled=True)  30.6 us
    all_to_all x1, waiting for transfers between devices, sum_at_owner(): lax.all_to_all(split_up(array, dim, devices), axis, 0, 0, tiled=True)  28.5 us
    all_to_all x1, starting transfers between devices, sum_at_owner(): lax.all_to_all(split_up(array, dim, devices), axis, 0, 0, tiled=True)  23.9 us
    all_gather x1, local copies, waits for them, and re-layouts, body(): lax.all_gather(right_factor, 'row', axis=0, tiled=True)  17.8 us
    dot_general x6, matrix products, attend(): jnp.einsum('ihjk,ikhd->ijhd', weights, value_block, preferred_element_typ...  14.3 us
    all_to_all x1, starting transfers between devices, from_everyone(): return lax.all_to_all(copies, axis, split_axis=0, concat_axis=0, tiled=True)  12.5 us
    dot_general x1, matrix products, body(): jnp.einsum('ikh,jkh->ijh', left_factor, lax.all_gather(right_factor, 'row...  9.08 us
  transfers between devices with their start and end apart: 5, of which 4 were waited for; matrix products, arithmetic and copies ran while one was open for 2% of the time, Pallas kernels for 0%

commit v1 on v0

v1 whole, which is shorter than its diff:
```python
import functools

import jax
import jax.numpy as jnp
from jax import lax
from jax.experimental import pallas as pl
from jax.experimental.pallas import tpu as pltpu
from jax.sharding import PartitionSpec as P

MESH = pl.DeviceIdType.MESH
EPSILON = 1e-05
MASK_PENALTY = 1000000000.0
F32 = jnp.float32
BF16 = jnp.bfloat16
CHUNKS = 4


def norm_last(values_in, gain):
    center = jnp.mean(values_in, axis=-1, keepdims=True)
    centered = values_in - center
    variance = jnp.mean(centered * centered, axis=-1, keepdims=True)
    return centered * lax.rsqrt(variance + EPSILON) * gain


def dot(a, b):
    return lax.dot_general(a, b, (((1,), (0,)), ((), ())), preferred_element_type=F32)


def dot_nt(a, b):
    return lax.dot_general(a, b, (((1,), (1,)), ((), ())), preferred_element_type=F32)


def one_hot(rows, cols, match):
    r = lax.broadcasted_iota(jnp.int32, (rows, cols), 0)
    c = lax.broadcasted_iota(jnp.int32, (rows, cols), 1)
    return jnp.where(match(r, c), 1.0, 0.0).astype(BF16)


def kernel(
    planes,
    groups,
    subs,
    heads,
    pair_ref,
    live_row_ref,
    live_col_ref,
    mask_ref,
    gain1_ref,
    w_in_ref,
    w_gate_ref,
    gain2_ref,
    w_tri_ref,
    gain3_ref,
    w_att_ref,
    w_bias_ref,
    w_out_ref,
    out_ref,
    right_buf,
    left_buf,
    normed_buf,
    part_buf,
    sum_buf,
    tmp_buf,
    tri_buf,
    att_buf,
    key_buf,
    value_buf,
    query_buf,
    gate_buf,
    score_buf,
    mid_buf,
    bias_rows,
    bias_z,
    bias_x,
    bias_buf,
    gated_buf,
    ring_send,
    ring_recv,
    part_send,
    part_recv,
    att_send,
    att_recv,
    bz_send,
    bz_recv,
    bx_send,
    bx_recv,
):
    rows, cols, chan = pair_ref.shape
    flat = rows * cols
    per_owner = planes // groups
    residues = groups * cols
    z = lax.axis_index("row")
    g = lax.axis_index(("col", "sub"))
    z_up = lax.rem(z + 1, planes)
    z_down = lax.rem(z + planes - 1, planes)

    def in_plane(c):
        return {"col": c // subs, "sub": lax.rem(c, subs)}

    barrier = pltpu.get_barrier_semaphore()
    for other in (z_up, z_down):
        pl.semaphore_signal(barrier, inc=1, device_id={"row": other}, device_id_type=MESH)
    for d in range(1, groups):
        pl.semaphore_signal(
            barrier, inc=1, device_id=in_plane(lax.rem(g + d, groups)), device_id_type=MESH
        )

    pair = pair_ref[...].reshape(flat, chan)
    normed = norm_last(pair, gain1_ref[...]).astype(BF16)
    normed_buf[...] = normed
    live_rows = live_row_ref[z]
    live_cols = live_col_ref[g]
    live = jnp.concatenate([live_rows[i : i + 1] * live_cols for i in range(rows)], axis=0)

    def factor(p):
        gate = dot(normed, w_in_ref[:, p * chan : (p + 1) * chan])
        value = dot(normed, w_in_ref[:, (p + 1) * chan : (p + 2) * chan])
        return (jax.nn.sigmoid(gate) * value * live).astype(BF16)

    right_buf[z] = factor(2).reshape(rows, cols, chan)
    pl.semaphore_wait(barrier, groups + 1)

    chunk_rows = rows // CHUNKS
    half = planes // 2
    last = half - 1

    def ring_copy(way, step, chunk):
        origin = lax.rem(z + planes - step, planes) if way == 0 else lax.rem(z + step, planes)
        block = right_buf.at[origin, pl.ds(chunk * chunk_rows, chunk_rows)]
        return pltpu.make_async_remote_copy(
            src_ref=block,
            dst_ref=block,
            send_sem=ring_send.at[way, step, chunk],
            recv_sem=ring_recv.at[way, step, chunk],
            device_id={"row": z_up if way == 0 else z_down},
            device_id_type=MESH,
        )

    def ring_arrival(way, step, chunk):
        origin = (
            lax.rem(z + 2 * planes - 1 - step, planes) if way == 0 else lax.rem(z + 1 + step, planes)
        )
        block = right_buf.at[origin, pl.ds(chunk * chunk_rows, chunk_rows)]
        pltpu.make_async_remote_copy(
            src_ref=block,
            dst_ref=block,
            send_sem=ring_send.at[way, step, chunk],
            recv_sem=ring_recv.at[way, step, chunk],
            device_id={"row": z_up if way == 0 else z_down},
            device_id_type=MESH,
        ).wait_recv()
        return origin

    halves = (range(CHUNKS // 2), range(CHUNKS // 2, CHUNKS))
    for chunk in range(CHUNKS):
        for way in range(2):
            ring_copy(way, 0, chunk).start()

    left_buf[...] = factor(0).astype(F32).reshape(rows, cols, chan)

    def products(origin, chunk):
        for j in range(chunk * chunk_rows, (chunk + 1) * chunk_rows):
            right = right_buf[origin, j].astype(F32)
            part_buf[origin, j * rows : (j + 1) * rows, :] = jnp.sum(
                left_buf[...] * right[None], axis=1
            )

    def part_copy(origin):
        owner = origin // per_owner
        return pltpu.make_async_remote_copy(
            src_ref=part_buf.at[origin],
            dst_ref=sum_buf.at[g, lax.rem(origin, per_owner)],
            send_sem=part_send.at[origin],
            recv_sem=part_recv.at[g, lax.rem(origin, per_owner)],
            device_id=in_plane(owner),
            device_id_type=MESH,
        )

    def to_owner(origin):
        @pl.when(origin // per_owner != g)
        def _():
            part_copy(origin).start()

    for chunk in range(CHUNKS):
        products(z, chunk)
    to_owner(z)

    def ring_step(step, carry):
        up = down = None
        for chunk in range(CHUNKS):
            for way in range(2):
                origin = ring_arrival(way, step, chunk)
                if chunk in halves[way]:
                    ring_copy(way, step + 1, chunk).start()
                else:

                    @pl.when(step + 1 < last)
                    def _():
                        ring_copy(way, step + 1, chunk).start()

                if way == 0:
                    up = origin
                else:
                    down = origin
            products(up, chunk)
            products(down, chunk)
        to_owner(up)
        to_owner(down)
        return carry

    lax.fori_loop(0, last, ring_step, 0)
    far = lax.rem(z + half, planes)
    for pair_of in zip(*halves):
        for way, chunk in enumerate(pair_of):
            ring_arrival(way, last, chunk)
            products(far, chunk)
    to_owner(far)

    tri_gate = jax.nn.sigmoid(dot(normed_buf[...], w_gate_ref[...]))

    block = rows * rows
    for p in range(per_owner):
        total = part_buf[g * per_owner + p]
        for d in range(1, groups):
            c = lax.rem(g + d, groups)
            pltpu.make_async_remote_copy(
                src_ref=part_buf.at[p],
                dst_ref=sum_buf.at[c, p],
                send_sem=part_send.at[p],
                recv_sem=part_recv.at[c, p],
                device_id=in_plane(c),
                device_id_type=MESH,
            ).wait_recv()
            total = total + sum_buf[c, p]
        tmp_buf[p * block : (p + 1) * block, :] = total
    for i in range(rows):
        tri_buf[i * cols : (i + 1) * cols, :] = tmp_buf[pl.ds(i, cols, stride=rows), :]

    hidden = norm_last(tri_buf[...], gain2_ref[...]).astype(BF16)
    pair_mid = pair_ref[...].reshape(flat, chan) + tri_gate * dot(hidden, w_tri_ref[...])
    mid_buf[...] = pair_mid
    att = norm_last(pair_mid, gain3_ref[...]).astype(BF16)
    att_buf[g] = att.reshape(rows, cols, chan)

    for j in range(rows):
        bias_rows[j * 8 : (j + 1) * 8, :] = dot_nt(
            w_bias_ref[...], att[j * cols : (j + 1) * cols, :]
        )
    packed_rows = bias_z.shape[1]
    half_rows = rows // 2
    stacked = bias_rows[...].astype(BF16)
    message = jnp.zeros((packed_rows, chan), F32)
    for q in range(2):
        pick = one_hot(
            packed_rows,
            rows * 8,
            lambda r, c: c == (q * half_rows + lax.rem(r, half_rows)) * 8 + r // half_rows,
        )
        spread = one_hot(cols, chan, lambda r, c: c == r + q * cols)
        message = message + dot(dot(pick, stacked).astype(BF16), spread)
    bias_z[z] = message.astype(BF16)

    def bz_copy(source, target):
        return pltpu.make_async_remote_copy(
            src_ref=bias_z.at[source],
            dst_ref=bias_z.at[source],
            send_sem=bz_send.at[target],
            recv_sem=bz_recv.at[source],
            device_id={"row": target},
            device_id_type=MESH,
        )

    def send_bias(k, carry):
        bz_copy(z, lax.rem(z + half + k, planes)).start()
        bz_copy(z, lax.rem(z + half - k, planes)).start()
        return carry

    bz_copy(z, lax.rem(z + half, planes)).start()
    lax.fori_loop(1, half, send_bias, 0)

    def att_copy(source, target):
        return pltpu.make_async_remote_copy(
            src_ref=att_buf.at[source],
            dst_ref=att_buf.at[source],
            send_sem=att_send.at[target],
            recv_sem=att_recv.at[source],
            device_id=in_plane(target),
            device_id_type=MESH,
        )

    for d in range(1, groups):
        att_copy(g, lax.rem(g + d, groups)).start()

    scale = (chan // heads) ** (-0.5)
    query_buf[...] = (dot(att, w_att_ref[:, :chan]) * scale).astype(BF16)
    gate_buf[...] = jax.nn.sigmoid(dot(att, w_att_ref[:, 3 * chan :]))

    for d in range(groups):
        c = lax.rem(g + d, groups)
        if d:
            att_copy(c, g).wait_recv()
        here = pl.ds(pl.multiple_of(c * cols, cols), cols)
        both = dot(att_buf[c].reshape(flat, chan), w_att_ref[:, chan : 3 * chan]).astype(BF16)
        key_buf[:, here, :] = both[:, :chan].reshape(rows, cols, chan)
        value_buf[:, here, :] = both[:, chan:].reshape(rows, cols, chan)

    lane_head = lax.broadcasted_iota(jnp.int32, (cols, chan), 1) // (chan // heads)

    def raw_scores(i, carry):
        query = query_buf[pl.ds(pl.multiple_of(i * cols, cols), cols), :]
        stack = jnp.concatenate(
            [jnp.where(lane_head == h, query, jnp.zeros_like(query)) for h in range(heads)], axis=0
        )
        score_buf[i] = dot_nt(stack, key_buf[i])
        return carry

    lax.fori_loop(0, rows, raw_scores, 0)

    def bx_copy(source, target):
        return pltpu.make_async_remote_copy(
            src_ref=bias_z.at[pl.ds(target * per_owner, per_owner)],
            dst_ref=bias_x.at[source],
            send_sem=bx_send.at[target],
            recv_sem=bx_recv.at[source],
            device_id=in_plane(target),
            device_id_type=MESH,
        )

    for d in range(groups):
        c = lax.rem(g + d, groups)
        for p in range(per_owner):
            source = c * per_owner + p

            @pl.when(source != z)
            def _():
                bz_copy(source, z).wait_recv()

        if d:
            bx_copy(g, c).start()

    sums = [jnp.zeros((per_owner * packed_rows, residues), F32) for _ in range(2)]
    for d in range(groups):
        c = lax.rem(g + d, groups)
        if d:
            bx_copy(c, g).wait_recv()
            piece = bias_x[c]
        else:
            piece = bias_z[pl.ds(g * per_owner, per_owner)]
        piece = piece.reshape(per_owner * packed_rows, chan)
        for q in range(2):
            spread = one_hot(
                chan, residues, lambda r, k: (k - c * cols == r - q * cols) & (r >= q * cols) & (r < (q + 1) * cols)
            )
            sums[q] = sums[q] + dot(piece, spread)
    bias = jnp.zeros((heads * cols, residues), F32)
    for q in range(2):
        def match(r, c):
            h, j = r // cols, lax.rem(r, cols)
            p, j = j // rows, lax.rem(j, rows)
            return (j // half_rows == q) & (
                c == p * packed_rows + h * half_rows + lax.rem(j, half_rows)
            )

        bias = bias + dot(
            one_hot(heads * cols, per_owner * packed_rows, match), sums[q].astype(BF16)
        )
    bias_buf[...] = bias + mask_ref[...]

    def attend(i, carry):
        scores = score_buf[i] + bias_buf[...]
        raised = jnp.exp(scores - jnp.max(scores, axis=-1, keepdims=True))
        weights = (raised * (1.0 / jnp.sum(raised, axis=-1, keepdims=True))).astype(BF16)
        mixed = dot(weights, value_buf[i])
        attended = jnp.zeros((cols, chan), F32)
        for h in range(heads):
            attended = jnp.where(lane_head == h, mixed[h * cols : (h + 1) * cols, :], attended)
        here = pl.ds(pl.multiple_of(i * cols, cols), cols)
        gated_buf[here, :] = (attended * gate_buf[here, :]).astype(BF16)
        return carry

    lax.fori_loop(0, rows, attend, 0)
    out_ref[...] = (mid_buf[...] + dot(gated_buf[...], w_out_ref[...])).reshape(rows, cols, chan)

    def ring_sent(step, carry):
        for way in range(2):
            for chunk in range(CHUNKS):
                ring_copy(way, step, chunk).wait_send()
        return carry

    lax.fori_loop(0, last, ring_sent, 0)
    for way in range(2):
        for chunk in halves[way]:
            ring_copy(way, last, chunk).wait_send()

    def parts_sent(origin, carry):
        @pl.when(origin // per_owner != g)
        def _():
            part_copy(origin).wait_send()

        @pl.when(origin != z)
        def _():
            bz_copy(z, origin).wait_send()

        return carry

    lax.fori_loop(0, planes, parts_sent, 0)
    for d in range(1, groups):
        c = lax.rem(g + d, groups)
        att_copy(g, c).wait_send()
        bx_copy(g, c).wait_send()


def solution(mesh):
    planes = mesh.shape["row"]
    subs = mesh.shape["sub"]
    groups = mesh.shape["col"] * subs

    def body(
        pair,
        residue_mask,
        tri_norm_gain,
        tri_in_weight,
        tri_gate_weight,
        tri_out_norm_gain,
        tri_out_weight,
        att_norm_gain,
        att_proj_weight,
        att_bias_weight,
        att_out_weight,
    ):
        rows, cols, chan = pair.shape
        heads = att_bias_weight.shape[1]
        residues = residue_mask.shape[0]
        live = residue_mask.astype(F32)
        live_row = jnp.broadcast_to(live.reshape(planes, rows, 1), (planes, rows, chan))
        live_col = jnp.broadcast_to(live.reshape(groups, cols, 1), (groups, cols, chan))
        mask_row = ((live - 1.0) * MASK_PENALTY)[None, :]
        w_bias = jnp.concatenate(
            [att_bias_weight.T, jnp.zeros((8 - heads, chan), att_bias_weight.dtype)], axis=0
        )
        flat = rows * cols
        per_owner = planes // groups
        packed = heads * rows // 2
        vmem = pl.BlockSpec(memory_space=pltpu.VMEM)
        dma = pltpu.SemaphoreType.DMA
        operands = (
            pair,
            live_row,
            live_col,
            mask_row,
            tri_norm_gain[None, :],
            tri_in_weight.reshape(chan, -1),
            tri_gate_weight,
            tri_out_norm_gain[None, :],
            tri_out_weight,
            att_norm_gain[None, :],
            att_proj_weight.reshape(chan, -1),
            w_bias,
            att_out_weight,
        )
        return pl.pallas_call(
            functools.partial(kernel, planes, groups, subs, heads),
            out_shape=jax.ShapeDtypeStruct(pair.shape, F32),
            in_specs=[vmem] * len(operands),
            out_specs=vmem,
            scratch_shapes=[
                pltpu.VMEM((planes, rows, cols, chan), BF16),
                pltpu.VMEM((rows, cols, chan), F32),
                pltpu.VMEM((flat, chan), BF16),
                pltpu.VMEM((planes, rows * rows, chan), F32),
                pltpu.VMEM((groups, per_owner, rows * rows, chan), F32),
                pltpu.VMEM((flat, chan), F32),
                pltpu.VMEM((flat, chan), F32),
                pltpu.VMEM((groups, rows, cols, chan), BF16),
                pltpu.VMEM((rows, residues, chan), BF16),
                pltpu.VMEM((rows, residues, chan), BF16),
                pltpu.VMEM((flat, chan), BF16),
                pltpu.VMEM((flat, chan), F32),
                pltpu.VMEM((rows, heads * cols, residues), F32),
                pltpu.VMEM((flat, chan), F32),
                pltpu.VMEM((rows * 8, cols), F32),
                pltpu.VMEM((planes, packed, chan), BF16),
                pltpu.VMEM((groups, per_owner, packed, chan), BF16),
                pltpu.VMEM((heads * cols, residues), F32),
                pltpu.VMEM((flat, chan), BF16),
                dma((2, planes // 2, CHUNKS)),
                dma((2, planes // 2, CHUNKS)),
                dma((planes,)),
                dma((groups, per_owner)),
                dma((groups,)),
                dma((groups,)),
                dma((planes,)),
                dma((planes,)),
                dma((groups,)),
                dma((groups,)),
            ],
            compiler_params=pltpu.CompilerParams(
                collective_id=0, has_side_effects=True, vmem_limit_bytes=56 * 1024 * 1024
            ),
            name="pair_update",
        )(*operands)

    placed = (P(("parts", "row"), ("col", "sub"), None), P("parts")) + (P(),) * 9
    return jax.shard_map(
        body,
        mesh=mesh,
        in_specs=placed,
        out_specs=P(("parts", "row"), ("col", "sub"), None),
        check_vma=False,
    )
```

time: 342 us -> 153 us (0.45)
  waiting for transfers between devices: 212 us -> 0 us
  Pallas kernels: 0 us -> 145 us
  starting transfers between devices: 42.3 us -> 0 us
  matrix products: 31.6 us -> 0 us
  local copies, waits for them, and re-layouts: 35.8 us -> 6.87 us
  between operations: 13.8 us -> 0.02 us
  other arithmetic: 5.57 us -> 0.01 us
    all_gather x2 -> x0, waiting for transfers between devices: 147 us -> none  [the longest x1 147 us: body(): lax.all_gather(right_factor, 'row', axis=0, tiled=True)]
    pallas_call x0 -> x1, Pallas kernels: none -> 145 us  [body(): pl.pallas_call(functools.partial(kernel, planes, groups, subs, heads), ou...]
    all_to_all x3 -> x0, waiting for transfers between devices: 64.2 us -> none  [the longest x1 30.6 us: from_everyone(): return lax.all_to_all(copies, axis, split_axis=0, concat_axis=0, tiled=True)]
    all_to_all x3 -> x0, starting transfers between devices: 42.3 us -> none  [the longest x1 23.9 us: sum_at_owner(): lax.all_to_all(split_up(array, dim, devices), axis, 0, 0, tiled=True)]
    dot_general x19 -> x0, matrix products: 28.9 us -> none  [the longest x6 14.3 us: attend(): jnp.einsum('ihjk,ikhd->ijhd', weights, value_block, preferred_element_typ...]
    all_gather x1 -> x0, local copies, waits for them, and re-layouts: 17.8 us -> none  [body(): lax.all_gather(right_factor, 'row', axis=0, tiled=True)]
    transpose x2 -> x0, local copies, waits for them, and re-layouts: 5.41 us -> none  [the longest x1 3.29 us: split_up(): return jnp.moveaxis(pieces, dim, 0)]
    split x3 -> x0, local copies, waits for them, and re-layouts: 3.92 us -> none  [in_one_piece(): jnp.split(result, [sum(widths[:k]) for k in range(1, len(widths))], axis=...]
  transfers between devices with their start and end apart: 5 -> 0, of which waited for: 4 -> 0; matrix products, arithmetic and copies ran while one was open for 2% -> 0% of each run, Pallas kernels for 0% -> 0%
where the time goes in v1:
time: 153 us; the launch traced here: 152 us
  Pallas kernels  145 us (95%)
  local copies, waits for them, and re-layouts  6.87 us (4%)
    pallas_call x1, Pallas kernels, body(): pl.pallas_call(functools.partial(kernel, planes, groups, subs, heads), ou...  145 us
    unnamed x9, local copies, waits for them, and re-layouts  3.18 us

profile of v1, /device:TPU:33, one launch (start us, length us, event | category | flops | bytes accessed | tf_op | source)
XLA Modules:
  0.0 151.7 jit_solution(5136256787919236085)
XLA Ops:
  0.0 0.0 copy-start.2
  0.0 0.7 copy-done.2
  0.7 0.0 copy-start.3
  0.7 0.7 copy-done.3
  1.4 0.6 concatenate.3.w_bias_ref
  1.9 0.6 broadcast_in_dim.31.mask_ref
  2.5 0.1 broadcast_in_dim.29
  2.6 0.1 broadcast_in_dim.27
  2.7 0.8 broadcast_in_dim.30.live_col_ref
  3.5 0.0 copy-start
  3.5 0.0 copy-start.1
  3.5 0.8 broadcast_in_dim.28.live_row_ref
  4.3 0.1 copy-done
  4.4 0.1 copy-done.1
  4.5 0.7 copy_bitcast_fusion
  5.2 144.8 %pair_update.1 = f32[12,48,128]{2,1,0:T(8,128)} custom-call(f32[12,48,128]{2,1,0:T(8,128)} %pair_ref.1, f32[32,12,128]{2,1,0:T(8,128)} %broadcast_in_dim.28.live_row_ref, f32[8,48,128]{2,1,0:T(8,128)} %broadcast_in_dim.30.live_col_ref, f32[1,384]{1,0:T(1,128)} %broadcast_in_dim.31.mask_ref, f32[1,128]{1,0:T(1,128)} %bitcast.13, ...), custom_call_target="tpu_custom_call" | custom-call | tf_op jit(solution)/shard_map/pair_update/pallas_call | solution.py:461
  150.0 1.7 %copy.17 = f32[12,48,128]{2,1,0:T(8,128)} copy(f32[12,48,128]{2,1,0:T(8,128)} %pair_update.1) | data formatting | bytes 589824
  (2 shorter events, 0.0 us)
Async XLA Ops:
  0.0 0.7 copy-start.2
  0.7 0.7 copy-start.3
  3.5 0.9 copy-start
  3.5 1.0 copy-start.1

commit v2 on v1

v2 whole, which is shorter than its diff:
```python
import functools

import jax
import jax.numpy as jnp
from jax import lax
from jax.experimental import pallas as pl
from jax.experimental.pallas import tpu as pltpu
from jax.sharding import PartitionSpec as P

MESH = pl.DeviceIdType.MESH
EPSILON = 1e-05
MASK_PENALTY = 1000000000.0
F32 = jnp.float32
BF16 = jnp.bfloat16
CHUNKS = 4
LAG = 4
STRIDE = 4


def norm_last(values_in, gain):
    center = jnp.mean(values_in, axis=-1, keepdims=True)
    centered = values_in - center
    variance = jnp.mean(centered * centered, axis=-1, keepdims=True)
    return centered * lax.rsqrt(variance + EPSILON) * gain


def dot(a, b):
    return lax.dot_general(a, b, (((1,), (0,)), ((), ())), preferred_element_type=F32)


def dot_nt(a, b):
    return lax.dot_general(a, b, (((1,), (1,)), ((), ())), preferred_element_type=F32)


def one_hot(rows, cols, match):
    r = lax.broadcasted_iota(jnp.int32, (rows, cols), 0)
    c = lax.broadcasted_iota(jnp.int32, (rows, cols), 1)
    return jnp.where(match(r, c), 1.0, 0.0).astype(BF16)


def kernel(
    planes,
    chips,
    subs,
    heads,
    pair_ref,
    mask_ref,
    gain1_ref,
    w_in_ref,
    w_gate_ref,
    gain2_ref,
    w_tri_ref,
    gain3_ref,
    w_att_ref,
    w_bias_ref,
    w_out_ref,
    out_ref,
    right_buf,
    left_buf,
    normed_buf,
    weight_buf,
    part_buf,
    sum_buf,
    tmp_buf,
    tri_buf,
    att_buf,
    key_buf,
    value_buf,
    query_buf,
    gate_buf,
    score_buf,
    mid_buf,
    bias_rows,
    bias_z,
    bias_x,
    bias_buf,
    gated_buf,
    ring_send,
    ring_recv,
    first_send,
    hand_send,
    hand_recv,
    part_send,
    part_recv,
    att_send,
    att_pass,
    att_recv,
    bz_far,
    bz_near,
    bz_recv,
    bx_send,
    bx_recv,
):
    rows, cols, chan = pair_ref.shape
    groups = chips * subs
    flat = rows * cols
    per_owner = planes // groups
    residues = groups * cols
    z = lax.axis_index("row")
    x = lax.axis_index("col")
    core = lax.axis_index("sub")
    g = x * subs + core
    mate = 1 - core
    ahead = lax.rem(z + planes + 2 * core - 1, planes)
    upper = lax.rem(z + 1, planes)
    lower = lax.rem(z + planes - 1, planes)

    def in_plane(c):
        return {"col": c // subs, "sub": lax.rem(c, subs)}

    barrier = pltpu.get_barrier_semaphore()
    for other in (upper, lower):
        for s in range(subs):
            pl.semaphore_signal(
                barrier, inc=1, device_id={"row": other, "sub": s}, device_id_type=MESH
            )
    for d in range(1, groups):
        pl.semaphore_signal(
            barrier, inc=1, device_id=in_plane(lax.rem(g + d, groups)), device_id_type=MESH
        )

    pair = pair_ref[...].reshape(flat, chan)
    normed = norm_last(pair, gain1_ref[...]).astype(BF16)
    normed_buf[...] = normed
    residue_live = mask_ref[...].reshape(1, residues).astype(F32)
    live_rows_of = jnp.broadcast_to(residue_live, (chan, residues)).astype(BF16)
    live_rows = dot_nt(one_hot(16, residues, lambda r, c: c == r + z * rows), live_rows_of)
    live_cols = dot_nt(one_hot(cols, residues, lambda r, c: c == r + g * cols), live_rows_of)
    live = jnp.concatenate([live_rows[i : i + 1] * live_cols for i in range(rows)], axis=0)
    weight_buf[...] = w_in_ref[...].astype(F32)

    def weight(p):
        return weight_buf[pl.ds(p, chan, stride=4), :].astype(BF16)

    def factor(p):
        gate = dot(normed, weight(p))
        value = dot(normed, weight(p + 1))
        return (jax.nn.sigmoid(gate) * value * live).astype(BF16)

    right_buf[z, core] = factor(2).reshape(rows, cols, chan)
    pl.semaphore_wait(barrier, 2 * subs + groups - 1)

    chunk_rows = rows // CHUNKS
    half = planes // 2
    last = half - 1

    def piece(origin, part, chunk):
        return right_buf.at[origin, part, pl.ds(chunk * chunk_rows, chunk_rows)]

    def behind(step):
        return lax.rem(z + 2 * planes - (2 * core - 1) * (1 + step), planes)

    def beyond(step):
        return lax.rem(z + 2 * planes + (2 * core - 1) * (1 + step), planes)

    def first_copy(way, chunk):
        return pltpu.make_async_remote_copy(
            src_ref=piece(z, core, chunk),
            dst_ref=piece(z, core, chunk),
            send_sem=first_send.at[way, chunk],
            recv_sem=ring_recv.at[0, core, chunk],
            device_id={"row": upper if way else lower, "sub": way},
            device_id_type=MESH,
        )

    def ring_copy(step, part, chunk):
        return pltpu.make_async_remote_copy(
            src_ref=piece(behind(step), part, chunk),
            dst_ref=piece(behind(step), part, chunk),
            send_sem=ring_send.at[step, part, chunk],
            recv_sem=ring_recv.at[step + 1, part, chunk],
            device_id={"row": ahead},
            device_id_type=MESH,
        )

    def ring_wait(step, part, chunk):
        block = piece(behind(step), part, chunk)
        pltpu.make_async_remote_copy(
            src_ref=block,
            dst_ref=block,
            send_sem=ring_send.at[0, part, chunk],
            recv_sem=ring_recv.at[step, part, chunk],
            device_id={"row": ahead},
            device_id_type=MESH,
        ).wait_recv()

    def hand_copy(step, chunk):
        block = piece(behind(step), mate, chunk)
        return pltpu.make_async_remote_copy(
            src_ref=block,
            dst_ref=block,
            send_sem=hand_send.at[step, chunk],
            recv_sem=hand_recv.at[step, chunk],
            device_id={"sub": mate},
            device_id_type=MESH,
        )

    def hand_wait(step, chunk):
        block = piece(beyond(step), core, chunk)
        pltpu.make_async_remote_copy(
            src_ref=block,
            dst_ref=block,
            send_sem=hand_send.at[step, chunk],
            recv_sem=hand_recv.at[step, chunk],
            device_id={"sub": mate},
            device_id_type=MESH,
        ).wait_recv()

    for chunk in range(CHUNKS):
        for way in range(2):
            first_copy(way, chunk).start()

    left_buf[...] = factor(0).astype(F32).reshape(rows, cols, chan)

    def products(origin, chunk):
        for j in range(chunk * chunk_rows, (chunk + 1) * chunk_rows):
            right = right_buf[origin, core, j].astype(F32)
            part_buf[origin, j * rows : (j + 1) * rows, :] = jnp.sum(
                left_buf[...] * right[None], axis=1
            )

    def part_copy(origin):
        owner = origin // per_owner
        return pltpu.make_async_remote_copy(
            src_ref=part_buf.at[origin],
            dst_ref=sum_buf.at[g, lax.rem(origin, per_owner)],
            send_sem=part_send.at[origin],
            recv_sem=part_recv.at[g, lax.rem(origin, per_owner)],
            device_id=in_plane(owner),
            device_id_type=MESH,
        )

    def to_owner(origin):
        @pl.when(origin // per_owner != g)
        def _():
            part_copy(origin).start()

    for chunk in range(CHUNKS):
        products(z, chunk)
    to_owner(z)
    weight_buf[...] = w_att_ref[...].astype(F32)

    far_chunks = CHUNKS // 2
    far_base = (1 - core) * far_chunks

    def handed(step):
        origin = beyond(step)
        for chunk in range(CHUNKS):
            hand_wait(step, chunk)
            products(origin, chunk)
        to_owner(origin)

    def ring_step(step, carry):
        origin = behind(step)
        for chunk in range(CHUNKS):
            wanted = (step + 1 < last) | (chunk // far_chunks == 1 - core)
            for part in range(subs):
                ring_wait(step, part, chunk)

                @pl.when(wanted)
                def _():
                    ring_copy(step, part, chunk).start()

            hand_copy(step, chunk).start()
            products(origin, chunk)
        to_owner(origin)

        @pl.when(step >= LAG)
        def _():
            handed(step - LAG)

        return carry

    lax.fori_loop(0, last, ring_step, 0)

    def late_step(step, carry):
        handed(step)
        return carry

    far = lax.rem(z + half, planes)
    for k in range(far_chunks):
        for part in range(subs):
            ring_wait(last, part, far_base + k)
        hand_copy(last, far_base + k).start()
    lax.fori_loop(max(last - LAG, 0), last, late_step, 0)
    for k in range(far_chunks):
        hand_wait(last, core * far_chunks + k)
    for chunk in range(CHUNKS):
        products(far, chunk)
    to_owner(far)

    tri_gate = jax.nn.sigmoid(dot(normed_buf[...], w_gate_ref[...]))

    block = rows * rows
    for p in range(per_owner):
        total = part_buf[g * per_owner + p]
        for d in range(1, groups):
            c = lax.rem(g + d, groups)
            pltpu.make_async_remote_copy(
                src_ref=part_buf.at[p],
                dst_ref=sum_buf.at[c, p],
                send_sem=part_send.at[p],
                recv_sem=part_recv.at[c, p],
                device_id=in_plane(c),
                device_id_type=MESH,
            ).wait_recv()
            total = total + sum_buf[c, p]
        tmp_buf[p * block : (p + 1) * block, :] = total
    for i in range(rows):
        tri_buf[i * cols : (i + 1) * cols, :] = tmp_buf[pl.ds(i, cols, stride=rows), :]

    hidden = norm_last(tri_buf[...], gain2_ref[...]).astype(BF16)
    pair_mid = pair_ref[...].reshape(flat, chan) + tri_gate * dot(hidden, w_tri_ref[...])
    mid_buf[...] = pair_mid
    att = norm_last(pair_mid, gain3_ref[...]).astype(BF16)
    att_buf[g] = att.reshape(rows, cols, chan)

    w_bias = jnp.concatenate(
        [w_bias_ref[...].astype(F32), jnp.zeros((8 - heads, chan), F32)], axis=0
    ).astype(BF16)

    for j in range(rows):
        bias_rows[j * 8 : (j + 1) * 8, :] = dot_nt(w_bias, att[j * cols : (j + 1) * cols, :])
    packed_rows = bias_z.shape[1]
    half_rows = rows // 2
    stacked = bias_rows[...].astype(BF16)
    message = jnp.zeros((packed_rows, chan), F32)
    for q in range(2):
        pick = one_hot(
            packed_rows,
            rows * 8,
            lambda r, c: c == (q * half_rows + lax.rem(r, half_rows)) * 8 + r // half_rows,
        )
        spread = one_hot(cols, chan, lambda r, c: c == r + q * cols)
        message = message + dot(dot(pick, stacked).astype(BF16), spread)
    bias_z[z] = message.astype(BF16)

    hops = planes // STRIDE
    near = (1, planes - 1, 2)

    def bz_copy(source, target, sem):
        return pltpu.make_async_remote_copy(
            src_ref=bias_z.at[source],
            dst_ref=bias_z.at[source],
            send_sem=sem,
            recv_sem=bz_recv.at[source],
            device_id={"row": target},
            device_id_type=MESH,
        )

    def bz_wait(source):
        bz_copy(source, z, bz_far.at[0]).wait_recv()

    def bz_far_copy(m):
        return bz_copy(z, lax.rem(z + STRIDE * m, planes), bz_far.at[m])

    def bz_near_copy(m, n):
        source = lax.rem(z + STRIDE * m, planes)
        return bz_copy(source, lax.rem(z + near[n], planes), bz_near.at[m, n])

    by_distance = sorted(range(1, hops), key=lambda m: min(m, hops - m))

    def pass_bias(m):
        if m:
            bz_wait(lax.rem(z + STRIDE * m, planes))
        for n in range(len(near)):
            bz_near_copy(m, n).start()

    for m in reversed(by_distance):
        bz_far_copy(m).start()
    pass_bias(0)

    def att_copy(source, target, sem):
        return pltpu.make_async_remote_copy(
            src_ref=att_buf.at[source],
            dst_ref=att_buf.at[source],
            send_sem=sem,
            recv_sem=att_recv.at[source],
            device_id=target,
            device_id_type=MESH,
        )

    def att_across(d):
        return att_copy(g, {"col": lax.rem(x + d, chips)}, att_send.at[d])

    def att_over(d):
        return att_copy(lax.rem(x + d, chips) * subs + core, {"sub": mate}, att_pass.at[d])

    for d in sorted(range(1, chips), key=lambda d: -min(d, chips - d)):
        att_across(d).start()
    att_over(0).start()

    def att_weight(p):
        return weight_buf[pl.ds(p, chan, stride=4), :].astype(BF16)

    scale = (chan // heads) ** (-0.5)
    query_buf[...] = (dot(att, att_weight(0)) * scale).astype(BF16)
    gate_buf[...] = jax.nn.sigmoid(dot(att, att_weight(3)))
    key_weight, value_weight = att_weight(1), att_weight(2)

    def key_value(c):
        here = pl.ds(pl.multiple_of(c * cols, cols), cols)
        normed_rows = att_buf[c].reshape(flat, chan)
        key_buf[:, here, :] = dot(normed_rows, key_weight).astype(BF16).reshape(rows, cols, chan)
        value_buf[:, here, :] = (
            dot(normed_rows, value_weight).astype(BF16).reshape(rows, cols, chan)
        )

    def att_wait(c):
        att_copy(c, {"sub": mate}, att_pass.at[0]).wait_recv()

    def ring_sent(step, carry):
        for chunk in range(CHUNKS):
            wanted = (step + 1 < last) | (chunk // far_chunks == 1 - core)

            @pl.when(wanted)
            def _():
                for part in range(subs):
                    ring_copy(step, part, chunk).wait_send()

            hand_copy(step, chunk).wait_send()
        return carry

    def parts_sent(origin, carry):
        @pl.when(origin // per_owner != g)
        def _():
            part_copy(origin).wait_send()

        return carry

    lax.fori_loop(0, last, ring_sent, 0)
    for k in range(far_chunks):
        hand_copy(last, far_base + k).wait_send()
    for chunk in range(CHUNKS):
        for way in range(2):
            first_copy(way, chunk).wait_send()
    lax.fori_loop(0, planes, parts_sent, 0)

    key_value(g)
    waiting = list(by_distance)
    for d in [0] + sorted(range(1, chips), key=lambda d: min(d, chips - d)):
        if d:
            c = lax.rem(x + d, chips) * subs + core
            att_wait(c)
            att_over(d).start()
            key_value(c)
        c = lax.rem(x + d, chips) * subs + mate
        att_wait(c)
        key_value(c)
        if len(waiting) > 2:
            for m in waiting[:2]:
                pass_bias(m)
            waiting = waiting[2:]

    lane_head = lax.broadcasted_iota(jnp.int32, (cols, chan), 1) // (chan // heads)

    def raw_scores(i, carry):
        query = query_buf[pl.ds(pl.multiple_of(i * cols, cols), cols), :]
        stack = jnp.concatenate(
            [jnp.where(lane_head == h, query, jnp.zeros_like(query)) for h in range(heads)], axis=0
        )
        score_buf[i] = dot_nt(stack, key_buf[i])
        return carry

    lax.fori_loop(0, rows, raw_scores, 0, unroll=2)
    for m in waiting:
        pass_bias(m)

    def bx_copy(source, target):
        return pltpu.make_async_remote_copy(
            src_ref=bias_z.at[pl.ds(target * per_owner, per_owner)],
            dst_ref=bias_x.at[source],
            send_sem=bx_send.at[target],
            recv_sem=bx_recv.at[source],
            device_id=in_plane(target),
            device_id_type=MESH,
        )

    for d in range(groups):
        c = lax.rem(g + d, groups)
        for p in range(per_owner):
            source = c * per_owner + p

            @pl.when(lax.rem(source + planes - z, STRIDE) != 0)
            def _():
                bz_wait(source)

        if d:
            bx_copy(g, c).start()

    sums = [jnp.zeros((per_owner * packed_rows, residues), F32) for _ in range(2)]
    for d in range(groups):
        c = lax.rem(g + d, groups)
        if d:
            bx_copy(c, g).wait_recv()
            piece = bias_x[c]
        else:
            piece = bias_z[pl.ds(g * per_owner, per_owner)]
        piece = piece.reshape(per_owner * packed_rows, chan)
        for q in range(2):
            spread = one_hot(
                chan, residues, lambda r, k: (k - c * cols == r - q * cols) & (r >= q * cols) & (r < (q + 1) * cols)
            )
            sums[q] = sums[q] + dot(piece, spread)
    bias = jnp.zeros((heads * cols, residues), F32)
    for q in range(2):
        def match(r, c):
            h, j = r // cols, lax.rem(r, cols)
            p, j = j // rows, lax.rem(j, rows)
            return (j // half_rows == q) & (
                c == p * packed_rows + h * half_rows + lax.rem(j, half_rows)
            )

        bias = bias + dot(
            one_hot(heads * cols, per_owner * packed_rows, match), sums[q].astype(BF16)
        )
    bias_buf[...] = bias + (residue_live - 1.0) * MASK_PENALTY

    def attend(i, carry):
        scores = score_buf[i] + bias_buf[...]
        raised = jnp.exp(scores - jnp.max(scores, axis=-1, keepdims=True))
        weights = (raised * (1.0 / jnp.sum(raised, axis=-1, keepdims=True))).astype(BF16)
        mixed = dot(weights, value_buf[i])
        attended = jnp.zeros((cols, chan), F32)
        for h in range(heads):
            attended = jnp.where(lane_head == h, mixed[h * cols : (h + 1) * cols, :], attended)
        here = pl.ds(pl.multiple_of(i * cols, cols), cols)
        gated_buf[here, :] = (attended * gate_buf[here, :]).astype(BF16)
        return carry

    lax.fori_loop(0, rows, attend, 0, unroll=2)
    out_ref[...] = (mid_buf[...] + dot(gated_buf[...], w_out_ref[...])).reshape(rows, cols, chan)

    for m in range(hops):
        if m:
            bz_far_copy(m).wait_send()
        for n in range(len(near)):
            bz_near_copy(m, n).wait_send()
    for d in range(chips):
        if d:
            att_across(d).wait_send()
        att_over(d).wait_send()
    for d in range(1, groups):
        bx_copy(g, lax.rem(g + d, groups)).wait_send()


def solution(mesh):
    planes = mesh.shape["row"]
    subs = mesh.shape["sub"]
    chips = mesh.shape["col"]
    groups = chips * subs

    def body(
        pair,
        residue_mask,
        tri_norm_gain,
        tri_in_weight,
        tri_gate_weight,
        tri_out_norm_gain,
        tri_out_weight,
        att_norm_gain,
        att_proj_weight,
        att_bias_weight,
        att_out_weight,
    ):
        rows, cols, chan = pair.shape
        heads = att_bias_weight.shape[1]
        residues = residue_mask.shape[0]
        flat = rows * cols
        per_owner = planes // groups
        packed = heads * rows // 2
        vmem = pl.BlockSpec(memory_space=pltpu.VMEM)
        dma = pltpu.SemaphoreType.DMA
        operands = (
            pair,
            residue_mask,
            tri_norm_gain[None, :],
            tri_in_weight.reshape(-1, chan),
            tri_gate_weight,
            tri_out_norm_gain[None, :],
            tri_out_weight,
            att_norm_gain[None, :],
            att_proj_weight.reshape(-1, chan),
            att_bias_weight.T,
            att_out_weight,
        )
        return pl.pallas_call(
            functools.partial(kernel, planes, chips, subs, heads),
            out_shape=jax.ShapeDtypeStruct(pair.shape, F32),
            in_specs=[vmem] * len(operands),
            out_specs=vmem,
            scratch_shapes=[
                pltpu.VMEM((planes, subs, rows, cols, chan), BF16),
                pltpu.VMEM((rows, cols, chan), F32),
                pltpu.VMEM((flat, chan), BF16),
                pltpu.VMEM((4 * chan, chan), F32),
                pltpu.VMEM((planes, rows * rows, chan), F32),
                pltpu.VMEM((groups, per_owner, rows * rows, chan), F32),
                pltpu.VMEM((flat, chan), F32),
                pltpu.VMEM((flat, chan), F32),
                pltpu.VMEM((groups, rows, cols, chan), BF16),
                pltpu.VMEM((rows, residues, chan), BF16),
                pltpu.VMEM((rows, residues, chan), BF16),
                pltpu.VMEM((flat, chan), BF16),
                pltpu.VMEM((flat, chan), F32),
                pltpu.VMEM((rows, heads * cols, residues), F32),
                pltpu.VMEM((flat, chan), F32),
                pltpu.VMEM((rows * 8, cols), F32),
                pltpu.VMEM((planes, packed, chan), BF16),
                pltpu.VMEM((groups, per_owner, packed, chan), BF16),
                pltpu.VMEM((heads * cols, residues), F32),
                pltpu.VMEM((flat, chan), BF16),
                dma((planes // 2, subs, CHUNKS)),
                dma((planes // 2, subs, CHUNKS)),
                dma((2, CHUNKS)),
                dma((planes // 2, CHUNKS)),
                dma((planes // 2, CHUNKS)),
                dma((planes,)),
                dma((groups, per_owner)),
                dma((chips,)),
                dma((chips,)),
                dma((groups,)),
                dma((planes // STRIDE,)),
                dma((planes // STRIDE, 3)),
                dma((planes,)),
                dma((groups,)),
                dma((groups,)),
            ],
            compiler_params=pltpu.CompilerParams(
                collective_id=0, has_side_effects=True, vmem_limit_bytes=56 * 1024 * 1024
            ),
            name="pair_update",
        )(*operands)

    placed = (P(("parts", "row"), ("col", "sub"), None), P("parts")) + (P(),) * 9
    return jax.shard_map(
        body,
        mesh=mesh,
        in_specs=placed,
        out_specs=P(("parts", "row"), ("col", "sub"), None),
        check_vma=False,
    )
```

time: 153 us -> 150 us (0.980)
  local copies, waits for them, and re-layouts: 6.87 us -> 1.69 us
  Pallas kernels: 145 us -> 148 us
    pallas_call x1, Pallas kernels: 145 us -> 148 us  [body(): pl.pallas_call(functools.partial(kernel, planes, chips, subs, heads), out...]
    broadcast_in_dim x5 -> x0, local copies, waits for them, and re-layouts: 2.39 us -> none  [the longest x2 0.94 us: body(): jnp.broadcast_to(live.reshape(planes, rows, 1), (planes, rows, chan))]
    unnamed x9 -> x1, local copies, waits for them, and re-layouts: 3.18 us -> 1.69 us
where the time goes in v2:
time: 150 us
  Pallas kernels  148 us (99%)
  local copies, waits for them, and re-layouts  1.69 us (1%)
    pallas_call x1, Pallas kernels, body(): pl.pallas_call(functools.partial(kernel, planes, chips, subs, heads), out...  148 us

profile of v2, /device:TPU:33, one launch (start us, length us, event | category | flops | bytes accessed | tf_op | source)
XLA Modules:
  0.0 149.8 jit_solution(13256886000445907564)
XLA Ops:
  0.0 148.1 %pair_update.1 = f32[12,48,128]{2,1,0:T(8,128)} custom-call(f32[12,48,128]{2,1,0:T(8,128)} %pair_ref.1, s32[384]{0:T(512)} %mask_ref.1, f32[1,128]{1,0:T(1,128)} %bitcast.9, bf16[512,128]{1,0:T(8,128)(2,1)} %bitcast.6, bf16[128,128]{1,0:T(8,128)(2,1)} %w_gate_ref.1, f32[1,128]{1,0:T(1,128)} %bitcast.10, bf16[128,128]{1,0:T(8,128)(2,1)} %w_tri_ref.1, ...), custom_call_target="tpu_custom_call" | custom-call | tf_op jit(solution)/shard_map/pair_update/pallas_call | solution.py:587
  148.1 1.7 %copy.13 = f32[12,48,128]{2,1,0:T(8,128)} copy(f32[12,48,128]{2,1,0:T(8,128)} %pair_update.1) | data formatting | bytes 589824

commit v3 on v2

--- a/solution.py
+++ b/solution.py
@@ -13,7 +13,6 @@
 F32 = jnp.float32
 BF16 = jnp.bfloat16
 CHUNKS = 4
-LAG = 4
 STRIDE = 4
 
 
@@ -56,6 +55,7 @@
     w_out_ref,
     out_ref,
     right_buf,
+    left_here,
     left_buf,
     normed_buf,
     weight_buf,
@@ -78,8 +78,9 @@
     ring_send,
     ring_recv,
     first_send,
-    hand_send,
-    hand_recv,
+    mate_send,
+    mate_recv,
+    mate_done,
     part_send,
     part_recv,
     att_send,
@@ -150,9 +151,6 @@
     def behind(step):
         return lax.rem(z + 2 * planes - (2 * core - 1) * (1 + step), planes)
 
-    def beyond(step):
-        return lax.rem(z + 2 * planes + (2 * core - 1) * (1 + step), planes)
-
     def first_copy(way, chunk):
         return pltpu.make_async_remote_copy(
             src_ref=piece(z, core, chunk),
@@ -184,76 +182,75 @@
             device_id_type=MESH,
         ).wait_recv()
 
-    def hand_copy(step, chunk):
-        block = piece(behind(step), mate, chunk)
+    def mate_copy(ref, k):
         return pltpu.make_async_remote_copy(
-            src_ref=block,
-            dst_ref=block,
-            send_sem=hand_send.at[step, chunk],
-            recv_sem=hand_recv.at[step, chunk],
+            src_ref=ref,
+            dst_ref=ref,
+            send_sem=mate_send.at[k],
+            recv_sem=mate_recv.at[k],
             device_id={"sub": mate},
             device_id_type=MESH,
         )
-
-    def hand_wait(step, chunk):
-        block = piece(beyond(step), core, chunk)
-        pltpu.make_async_remote_copy(
-            src_ref=block,
-            dst_ref=block,
-            send_sem=hand_send.at[step, chunk],
-            recv_sem=hand_recv.at[step, chunk],
-            device_id={"sub": mate},
-            device_id_type=MESH,
-        ).wait_recv()
 
     for chunk in range(CHUNKS):
         for way in range(2):
             first_copy(way, chunk).start()
-
-    left_buf[...] = factor(0).astype(F32).reshape(rows, cols, chan)
-
-    def products(origin, chunk):
-        for j in range(chunk * chunk_rows, (chunk + 1) * chunk_rows):
-            right = right_buf[origin, core, j].astype(F32)
-            part_buf[origin, j * rows : (j + 1) * rows, :] = jnp.sum(
-                left_buf[...] * right[None], axis=1
-            )
-
-    def part_copy(origin):
-        owner = origin // per_owner
+    mate_copy(right_buf.at[z, core], 0).start()
+    left = factor(0)
+    left_here[core] = left.reshape(rows, cols, chan)
+    mate_copy(left_here.at[core], 1).start()
+    left_buf[core] = left.astype(F32).reshape(rows, cols, chan)
+    weight_buf[...] = w_att_ref[...].astype(F32)
+
+    side = 1 - core
+    half_chunks = CHUNKS // 2
+
+    def products(origin, h, first, chunk):
+        for j in range(chunk_rows):
+            total = jnp.zeros((rows, chan), F32)
+            for part in range(subs):
+                right = right_buf[origin, part, (first + chunk) * chunk_rows + j].astype(F32)
+                total = total + jnp.sum(left_buf[part] * right[None], axis=1)
+            row = (chunk * chunk_rows + j) * rows
+            part_buf[origin, h, row : row + rows, :] = total
+
+    def part_copy(origin, h):
         return pltpu.make_async_remote_copy(
-            src_ref=part_buf.at[origin],
-            dst_ref=sum_buf.at[g, lax.rem(origin, per_owner)],
-            send_sem=part_send.at[origin],
-            recv_sem=part_recv.at[g, lax.rem(origin, per_owner)],
-            device_id=in_plane(owner),
-            device_id_type=MESH,
-        )
-
-    def to_owner(origin):
-        @pl.when(origin // per_owner != g)
+            src_ref=part_buf.at[origin, h],
+            dst_ref=sum_buf.at[x, lax.rem(origin, per_owner), h],
+            send_sem=part_send.at[origin, h],
+            recv_sem=part_recv.at[x, lax.rem(origin, per_owner), h],
+            device_id=in_plane(origin // per_owner),
+            device_id_type=MESH,
+        )
+
+    def to_owner(origin, h):
+        mine = origin // per_owner == g
+
+        @pl.when(jnp.logical_not(mine))
         def _():
-            part_copy(origin).start()
-
-    for chunk in range(CHUNKS):
-        products(z, chunk)
-    to_owner(z)
-    weight_buf[...] = w_att_ref[...].astype(F32)
-
-    far_chunks = CHUNKS // 2
-    far_base = (1 - core) * far_chunks
-
-    def handed(step):
-        origin = beyond(step)
-        for chunk in range(CHUNKS):
-            hand_wait(step, chunk)
-            products(origin, chunk)
-        to_owner(origin)
+            part_copy(origin, h).start()
+
+        @pl.when(mine)
+        def _():
+            sum_buf[x, lax.rem(origin, per_owner), h] = part_buf[origin, h]
+
+    def takes(origin, h):
+        gap = lax.rem(z + planes - origin, planes)
+        shared = (gap == 0) | (gap == half)
+        return (shared & (side == h)) | (jnp.logical_not(shared) & ((gap < half) == (core == 1)))
+
+    mate_copy(right_buf.at[z, mate], 0).wait_recv()
+    mate_copy(left_here.at[mate], 1).wait_recv()
+    left_buf[mate] = left_here[mate].astype(F32)
+    for chunk in range(half_chunks):
+        products(z, side, side * half_chunks, chunk)
+    to_owner(z, side)
 
     def ring_step(step, carry):
         origin = behind(step)
         for chunk in range(CHUNKS):
-            wanted = (step + 1 < last) | (chunk // far_chunks == 1 - core)
+            wanted = (step + 1 < last) | (chunk // half_chunks == side)
             for part in range(subs):
                 ring_wait(step, part, chunk)
 
@@ -261,51 +258,46 @@
                 def _():
                     ring_copy(step, part, chunk).start()
 
-            hand_copy(step, chunk).start()
-            products(origin, chunk)
-        to_owner(origin)
-
-        @pl.when(step >= LAG)
-        def _():
-            handed(step - LAG)
-
+            h = chunk // half_chunks
+            products(origin, h, h * half_chunks, chunk % half_chunks)
+            if chunk % half_chunks == half_chunks - 1:
+                to_owner(origin, h)
         return carry
 
     lax.fori_loop(0, last, ring_step, 0)
-
-    def late_step(step, carry):
-        handed(step)
-        return carry
-
     far = lax.rem(z + half, planes)
-    for k in range(far_chunks):
+    for k in range(half_chunks):
         for part in range(subs):
-            ring_wait(last, part, far_base + k)
-        hand_copy(last, far_base + k).start()
-    lax.fori_loop(max(last - LAG, 0), last, late_step, 0)
-    for k in range(far_chunks):
-        hand_wait(last, core * far_chunks + k)
-    for chunk in range(CHUNKS):
-        products(far, chunk)
-    to_owner(far)
+            ring_wait(last, part, side * half_chunks + k)
+        products(far, side, side * half_chunks, k)
+    to_owner(far, side)
+    pl.semaphore_signal(mate_done, inc=1, device_id={"sub": mate}, device_id_type=MESH)
 
     tri_gate = jax.nn.sigmoid(dot(normed_buf[...], w_gate_ref[...]))
 
     block = rows * rows
     for p in range(per_owner):
-        total = part_buf[g * per_owner + p]
-        for d in range(1, groups):
-            c = lax.rem(g + d, groups)
-            pltpu.make_async_remote_copy(
-                src_ref=part_buf.at[p],
-                dst_ref=sum_buf.at[c, p],
-                send_sem=part_send.at[p],
-                recv_sem=part_recv.at[c, p],
-                device_id=in_plane(c),
-                device_id_type=MESH,
-            ).wait_recv()
-            total = total + sum_buf[c, p]
-        tmp_buf[p * block : (p + 1) * block, :] = total
+        origin = g * per_owner + p
+        for h in range(2):
+            for d in range(chips):
+                chip = lax.rem(x + d, chips)
+
+                @pl.when(jnp.logical_not(takes(origin, h)) if d == 0 else chip >= 0)
+                def _():
+                    pltpu.make_async_remote_copy(
+                        src_ref=part_buf.at[0, h],
+                        dst_ref=sum_buf.at[chip, p, h],
+                        send_sem=part_send.at[0, h],
+                        recv_sem=part_recv.at[chip, p, h],
+                        device_id=in_plane(g),
+                        device_id_type=MESH,
+                    ).wait_recv()
+
+            total = sum_buf[0, p, h]
+            for chip in range(1, chips):
+                total = total + sum_buf[chip, p, h]
+            at = p * block + h * (block // 2)
+            tmp_buf[at : at + block // 2, :] = total
     for i in range(rows):
         tri_buf[i * cols : (i + 1) * cols, :] = tmp_buf[pl.ds(i, cols, stride=rows), :]
 
@@ -366,6 +358,7 @@
         for n in range(len(near)):
             bz_near_copy(m, n).start()
 
+    pl.semaphore_wait(mate_done, 1)
     for m in reversed(by_distance):
         bz_far_copy(m).start()
     pass_bias(0)
@@ -411,29 +404,30 @@
 
     def ring_sent(step, carry):
         for chunk in range(CHUNKS):
-            wanted = (step + 1 < last) | (chunk // far_chunks == 1 - core)
+            wanted = (step + 1 < last) | (chunk // half_chunks == side)
 
             @pl.when(wanted)
             def _():
                 for part in range(subs):
                     ring_copy(step, part, chunk).wait_send()
 
-            hand_copy(step, chunk).wait_send()
         return carry
 
     def parts_sent(origin, carry):
-        @pl.when(origin // per_owner != g)
-        def _():
-            part_copy(origin).wait_send()
+        for h in range(2):
+
+            @pl.when(takes(origin, h) & (origin // per_owner != g))
+            def _():
+                part_copy(origin, h).wait_send()
 
         return carry
 
     lax.fori_loop(0, last, ring_sent, 0)
-    for k in range(far_chunks):
-        hand_copy(last, far_base + k).wait_send()
     for chunk in range(CHUNKS):
         for way in range(2):
             first_copy(way, chunk).wait_send()
+    mate_copy(right_buf.at[z, core], 0).wait_send()
+    mate_copy(left_here.at[core], 1).wait_send()
     lax.fori_loop(0, planes, parts_sent, 0)
 
     key_value(g)
@@ -591,11 +585,12 @@
             out_specs=vmem,
             scratch_shapes=[
                 pltpu.VMEM((planes, subs, rows, cols, chan), BF16),
-                pltpu.VMEM((rows, cols, chan), F32),
+                pltpu.VMEM((subs, rows, cols, chan), BF16),
+                pltpu.VMEM((subs, rows, cols, chan), F32),
                 pltpu.VMEM((flat, chan), BF16),
                 pltpu.VMEM((4 * chan, chan), F32),
-                pltpu.VMEM((planes, rows * rows, chan), F32),
-                pltpu.VMEM((groups, per_owner, rows * rows, chan), F32),
+                pltpu.VMEM((planes, 2, rows * rows // 2, chan), F32),
+                pltpu.VMEM((chips, per_owner, 2, rows * rows // 2, chan), F32),
                 pltpu.VMEM((flat, chan), F32),
                 pltpu.VMEM((flat, chan), F32),
                 pltpu.VMEM((groups, rows, cols, chan), BF16),
@@ -613,10 +608,11 @@
                 dma((planes // 2, subs, CHUNKS)),
                 dma((planes // 2, subs, CHUNKS)),
                 dma((2, CHUNKS)),
-                dma((planes // 2, CHUNKS)),
-                dma((planes // 2, CHUNKS)),
-                dma((planes,)),
-                dma((groups, per_owner)),
+                dma((2,)),
+                dma((2,)),
+                pltpu.SemaphoreType.REGULAR,
+                dma((planes, 2)),
+                dma((chips, per_owner, 2)),
                 dma((chips,)),
                 dma((chips,)),
                 dma((groups,)),

time: 150 us -> 137 us (0.913)
  Pallas kernels: 148 us -> 134 us
    pallas_call x1, Pallas kernels: 148 us -> 134 us  [body(): pl.pallas_call(functools.partial(kernel, planes, chips, subs, heads), out...]
where the time goes in v3:
time: 137 us; the launch traced here: 136 us
  Pallas kernels  134 us (98%)
  local copies, waits for them, and re-layouts  1.69 us (1%)
    pallas_call x1, Pallas kernels, body(): pl.pallas_call(functools.partial(kernel, planes, chips, subs, heads), out...  134 us

profile of v3, /device:TPU:33, one launch (start us, length us, event | category | flops | bytes accessed | tf_op | source)
XLA Modules:
  0.0 136.0 jit_solution(4037533555325927001)
XLA Ops:
  0.0 134.3 %pair_update.1 = f32[12,48,128]{2,1,0:T(8,128)} custom-call(f32[12,48,128]{2,1,0:T(8,128)} %pair_ref.1, s32[384]{0:T(512)} %mask_ref.1, f32[1,128]{1,0:T(1,128)} %bitcast.9, bf16[512,128]{1,0:T(8,128)(2,1)} %bitcast.6, bf16[128,128]{1,0:T(8,128)(2,1)} %w_gate_ref.1, f32[1,128]{1,0:T(1,128)} %bitcast.10, bf16[128,128]{1,0:T(8,128)(2,1)} %w_tri_ref.1, ...), custom_call_target="tpu_custom_call" | custom-call | tf_op jit(solution)/shard_map/pair_update/pallas_call | solution.py:581
  134.3 1.7 %copy.13 = f32[12,48,128]{2,1,0:T(8,128)} copy(f32[12,48,128]{2,1,0:T(8,128)} %pair_update.1) | data formatting | bytes 589824

commit v4 on v3

--- a/solution.py
+++ b/solution.py
@@ -59,6 +59,7 @@
     left_buf,
     normed_buf,
     weight_buf,
+    stage_buf,
     part_buf,
     sum_buf,
     tmp_buf,
@@ -81,6 +82,7 @@
     mate_send,
     mate_recv,
     mate_done,
+    plane_done,
     part_send,
     part_recv,
     att_send,
@@ -89,7 +91,6 @@
     bz_far,
     bz_near,
     bz_recv,
-    bx_send,
     bx_recv,
 ):
     rows, cols, chan = pair_ref.shape
@@ -205,14 +206,14 @@
     side = 1 - core
     half_chunks = CHUNKS // 2
 
-    def products(origin, h, first, chunk):
+    def products(origin, first, chunk):
         for j in range(chunk_rows):
             total = jnp.zeros((rows, chan), F32)
             for part in range(subs):
                 right = right_buf[origin, part, (first + chunk) * chunk_rows + j].astype(F32)
                 total = total + jnp.sum(left_buf[part] * right[None], axis=1)
             row = (chunk * chunk_rows + j) * rows
-            part_buf[origin, h, row : row + rows, :] = total
+            stage_buf[row : row + rows, :] = total
 
     def part_copy(origin, h):
         return pltpu.make_async_remote_copy(
@@ -229,11 +230,12 @@
 
         @pl.when(jnp.logical_not(mine))
         def _():
+            part_buf[origin, h] = stage_buf[...]
             part_copy(origin, h).start()
 
         @pl.when(mine)
         def _():
-            sum_buf[x, lax.rem(origin, per_owner), h] = part_buf[origin, h]
+            sum_buf[x, lax.rem(origin, per_owner), h] = stage_buf[...]
 
     def takes(origin, h):
         gap = lax.rem(z + planes - origin, planes)
@@ -244,7 +246,7 @@
     mate_copy(left_here.at[mate], 1).wait_recv()
     left_buf[mate] = left_here[mate].astype(F32)
     for chunk in range(half_chunks):
-        products(z, side, side * half_chunks, chunk)
+        products(z, side * half_chunks, chunk)
     to_owner(z, side)
 
     def ring_step(step, carry):
@@ -259,7 +261,7 @@
                     ring_copy(step, part, chunk).start()
 
             h = chunk // half_chunks
-            products(origin, h, h * half_chunks, chunk % half_chunks)
+            products(origin, h * half_chunks, chunk % half_chunks)
             if chunk % half_chunks == half_chunks - 1:
                 to_owner(origin, h)
         return carry
@@ -269,9 +271,13 @@
     for k in range(half_chunks):
         for part in range(subs):
             ring_wait(last, part, side * half_chunks + k)
-        products(far, side, side * half_chunks, k)
+        products(far, side * half_chunks, k)
     to_owner(far, side)
     pl.semaphore_signal(mate_done, inc=1, device_id={"sub": mate}, device_id_type=MESH)
+    for d in range(1, groups):
+        pl.semaphore_signal(
+            plane_done, inc=1, device_id=in_plane(lax.rem(g + d, groups)), device_id_type=MESH
+        )
 
     tri_gate = jax.nn.sigmoid(dot(normed_buf[...], w_gate_ref[...]))
 
@@ -328,7 +334,7 @@
     bias_z[z] = message.astype(BF16)
 
     hops = planes // STRIDE
-    near = (1, planes - 1, 2)
+    near = (1, planes - 1, 2, 0)
 
     def bz_copy(source, target, sem):
         return pltpu.make_async_remote_copy(
@@ -348,7 +354,17 @@
 
     def bz_near_copy(m, n):
         source = lax.rem(z + STRIDE * m, planes)
-        return bz_copy(source, lax.rem(z + near[n], planes), bz_near.at[m, n])
+        return pltpu.make_async_remote_copy(
+            src_ref=bias_z.at[source],
+            dst_ref=bias_x.at[g, lax.rem(source, per_owner)],
+            send_sem=bz_near.at[m, n],
+            recv_sem=bx_recv.at[g, lax.rem(source, per_owner)],
+            device_id={"row": lax.rem(z + near[n], planes), **in_plane(source // per_owner)},
+            device_id_type=MESH,
+        )
+
+    def leaves(m, n):
+        return (lax.rem(z + STRIDE * m, planes) // per_owner != g) if near[n] == 0 else g >= 0
 
     by_distance = sorted(range(1, hops), key=lambda m: min(m, hops - m))
 
@@ -356,11 +372,21 @@
         if m:
             bz_wait(lax.rem(z + STRIDE * m, planes))
         for n in range(len(near)):
-            bz_near_copy(m, n).start()
+
+            @pl.when(leaves(m, n))
+            def _():
+                bz_near_copy(m, n).start()
+
+        source = lax.rem(z + STRIDE * m, planes)
+
+        @pl.when(source // per_owner == g)
+        def _():
+            bias_x[g, lax.rem(source, per_owner)] = bias_z[source]
 
     pl.semaphore_wait(mate_done, 1)
     for m in reversed(by_distance):
         bz_far_copy(m).start()
+    pl.semaphore_wait(plane_done, groups - 1)
     pass_bias(0)
 
     def att_copy(source, target, sem):
@@ -460,37 +486,27 @@
     for m in waiting:
         pass_bias(m)
 
-    def bx_copy(source, target):
-        return pltpu.make_async_remote_copy(
-            src_ref=bias_z.at[pl.ds(target * per_owner, per_owner)],
-            dst_ref=bias_x.at[source],
-            send_sem=bx_send.at[target],
-            recv_sem=bx_recv.at[source],
-            device_id=in_plane(target),
-            device_id_type=MESH,
-        )
-
     for d in range(groups):
         c = lax.rem(g + d, groups)
         for p in range(per_owner):
-            source = c * per_owner + p
-
-            @pl.when(lax.rem(source + planes - z, STRIDE) != 0)
+            source = g * per_owner + p
+            came = (lax.rem(source + planes - z, STRIDE) != 0) if d == 0 else c >= 0
+
+            @pl.when(came)
             def _():
-                bz_wait(source)
-
-        if d:
-            bx_copy(g, c).start()
+                pltpu.make_async_remote_copy(
+                    src_ref=bias_z.at[0],
+                    dst_ref=bias_x.at[c, p],
+                    send_sem=bz_near.at[0, 0],
+                    recv_sem=bx_recv.at[c, p],
+                    device_id=in_plane(g),
+                    device_id_type=MESH,
+                ).wait_recv()
 
     sums = [jnp.zeros((per_owner * packed_rows, residues), F32) for _ in range(2)]
     for d in range(groups):
         c = lax.rem(g + d, groups)
-        if d:
-            bx_copy(c, g).wait_recv()
-            piece = bias_x[c]
-        else:
-            piece = bias_z[pl.ds(g * per_owner, per_owner)]
-        piece = piece.reshape(per_owner * packed_rows, chan)
+        piece = bias_x[c].reshape(per_owner * packed_rows, chan)
         for q in range(2):
             spread = one_hot(
                 chan, residues, lambda r, k: (k - c * cols == r - q * cols) & (r >= q * cols) & (r < (q + 1) * cols)
@@ -529,13 +545,15 @@
         if m:
             bz_far_copy(m).wait_send()
         for n in range(len(near)):
-            bz_near_copy(m, n).wait_send()
+
+            @pl.when(leaves(m, n))
+            def _():
+                bz_near_copy(m, n).wait_send()
+
     for d in range(chips):
         if d:
             att_across(d).wait_send()
         att_over(d).wait_send()
-    for d in range(1, groups):
-        bx_copy(g, lax.rem(g + d, groups)).wait_send()
 
 
 def solution(mesh):
@@ -589,6 +607,7 @@
                 pltpu.VMEM((subs, rows, cols, chan), F32),
                 pltpu.VMEM((flat, chan), BF16),
                 pltpu.VMEM((4 * chan, chan), F32),
+                pltpu.VMEM((rows * rows // 2, chan), F32),
                 pltpu.VMEM((planes, 2, rows * rows // 2, chan), F32),
                 pltpu.VMEM((chips, per_owner, 2, rows * rows // 2, chan), F32),
                 pltpu.VMEM((flat, chan), F32),
@@ -611,16 +630,16 @@
                 dma((2,)),
                 dma((2,)),
                 pltpu.SemaphoreType.REGULAR,
+                pltpu.SemaphoreType.REGULAR,
                 dma((planes, 2)),
                 dma((chips, per_owner, 2)),
                 dma((chips,)),
                 dma((chips,)),
                 dma((groups,)),
                 dma((planes // STRIDE,)),
-                dma((planes // STRIDE, 3)),
+                dma((planes // STRIDE, 4)),
                 dma((planes,)),
-                dma((groups,)),
-                dma((groups,)),
+                dma((groups, per_owner)),
             ],
             compiler_params=pltpu.CompilerParams(
                 collective_id=0, has_side_effects=True, vmem_limit_bytes=56 * 1024 * 1024

time: 137 us -> 132 us (0.964)
  the two profiles are of different devices: /device:TPU:33 before, /device:TPU:35 now
where the time goes in v4:
time: 132 us
  Pallas kernels  131 us (99%)
  local copies, waits for them, and re-layouts  1.69 us (1%)
    pallas_call x1, Pallas kernels, body(): pl.pallas_call(functools.partial(kernel, planes, chips, subs, heads), out...  131 us

profile of v4, /device:TPU:35, one launch (start us, length us, event | category | flops | bytes accessed | tf_op | source)
XLA Modules:
  0.0 132.2 jit_solution(10295970300557598270)
XLA Ops:
  0.0 130.5 %pair_update.1 = f32[12,48,128]{2,1,0:T(8,128)} custom-call(f32[12,48,128]{2,1,0:T(8,128)} %pair_ref.1, s32[384]{0:T(512)} %mask_ref.1, f32[1,128]{1,0:T(1,128)} %bitcast.9, bf16[512,128]{1,0:T(8,128)(2,1)} %bitcast.6, bf16[128,128]{1,0:T(8,128)(2,1)} %w_gate_ref.1, f32[1,128]{1,0:T(1,128)} %bitcast.10, bf16[128,128]{1,0:T(8,128)(2,1)} %w_tri_ref.1, ...), custom_call_target="tpu_custom_call" | custom-call | tf_op jit(solution)/shard_map/pair_update/pallas_call | solution.py:599
  130.5 1.7 %copy.13 = f32[12,48,128]{2,1,0:T(8,128)} copy(f32[12,48,128]{2,1,0:T(8,128)} %pair_update.1) | data formatting | bytes 589824

commit v5 on v4

--- a/solution.py
+++ b/solution.py
@@ -14,6 +14,7 @@
 BF16 = jnp.bfloat16
 CHUNKS = 4
 STRIDE = 4
+LAG = 2
 
 
 def norm_last(values_in, gain):
@@ -61,6 +62,7 @@
     weight_buf,
     stage_buf,
     part_buf,
+    relay_buf,
     sum_buf,
     tmp_buf,
     tri_buf,
@@ -84,6 +86,7 @@
     mate_done,
     plane_done,
     part_send,
+    relay_recv,
     part_recv,
     att_send,
     att_pass,
@@ -225,17 +228,50 @@
             device_id_type=MESH,
         )
 
+    relayed = chips == 4
+
+    def away(origin):
+        return lax.rem(x + chips - origin // per_owner // subs, chips)
+
+    def relays(origin, h):
+        return (away(origin) == 1 + 2 * h) & relayed
+
+    def relay_copy(origin, h):
+        return pltpu.make_async_remote_copy(
+            src_ref=part_buf.at[origin, h],
+            dst_ref=relay_buf.at[origin, h],
+            send_sem=part_send.at[origin, h],
+            recv_sem=relay_recv.at[origin, h],
+            device_id={"col": lax.rem(x + chips + 2 * h - 1, chips)},
+            device_id_type=MESH,
+        )
+
     def to_owner(origin, h):
         mine = origin // per_owner == g
+        opposite = (away(origin) == 2) & relayed
+
+        @pl.when(mine)
+        def _():
+            sum_buf[x, lax.rem(origin, per_owner), h] = stage_buf[...]
 
         @pl.when(jnp.logical_not(mine))
         def _():
             part_buf[origin, h] = stage_buf[...]
+
+        @pl.when(opposite)
+        def _():
+            relay_copy(origin, h).start()
+
+        @pl.when(jnp.logical_not(mine | opposite | relays(origin, h)))
+        def _():
             part_copy(origin, h).start()
 
-        @pl.when(mine)
+    def relay(origin, h):
+        @pl.when(relays(origin, h))
         def _():
-            sum_buf[x, lax.rem(origin, per_owner), h] = stage_buf[...]
+            relay_copy(origin, h).wait_recv()
+            part_buf[origin, h] = part_buf[origin, h] + relay_buf[origin, h]
+            part_copy(origin, h).start()
 
     def takes(origin, h):
         gap = lax.rem(z + planes - origin, planes)
@@ -264,6 +300,17 @@
             products(origin, h * half_chunks, chunk % half_chunks)
             if chunk % half_chunks == half_chunks - 1:
                 to_owner(origin, h)
+        if relayed:
+
+            @pl.when(step == 1)
+            def _():
+                relay(z, side)
+
+            @pl.when(step >= LAG)
+            def _():
+                for h in range(2):
+                    relay(behind(step - LAG), h)
+
         return carry
 
     lax.fori_loop(0, last, ring_step, 0)
@@ -273,6 +320,11 @@
             ring_wait(last, part, side * half_chunks + k)
         products(far, side * half_chunks, k)
     to_owner(far, side)
+    if relayed:
+        for step in range(last - LAG, last):
+            for h in range(2):
+                relay(behind(step), h)
+        relay(far, side)
     pl.semaphore_signal(mate_done, inc=1, device_id={"sub": mate}, device_id_type=MESH)
     for d in range(1, groups):
         pl.semaphore_signal(
@@ -281,11 +333,12 @@
 
     tri_gate = jax.nn.sigmoid(dot(normed_buf[...], w_gate_ref[...]))
 
+    givers = (0, 1, 3) if relayed else tuple(range(chips))
     block = rows * rows
     for p in range(per_owner):
         origin = g * per_owner + p
         for h in range(2):
-            for d in range(chips):
+            for d in givers:
                 chip = lax.rem(x + d, chips)
 
                 @pl.when(jnp.logical_not(takes(origin, h)) if d == 0 else chip >= 0)
@@ -299,9 +352,9 @@
                         device_id_type=MESH,
                     ).wait_recv()
 
-            total = sum_buf[0, p, h]
-            for chip in range(1, chips):
-                total = total + sum_buf[chip, p, h]
+            total = sum_buf[x, p, h]
+            for d in givers[1:]:
+                total = total + sum_buf[lax.rem(x + d, chips), p, h]
             at = p * block + h * (block // 2)
             tmp_buf[at : at + block // 2, :] = total
     for i in range(rows):
@@ -609,6 +662,7 @@
                 pltpu.VMEM((4 * chan, chan), F32),
                 pltpu.VMEM((rows * rows // 2, chan), F32),
                 pltpu.VMEM((planes, 2, rows * rows // 2, chan), F32),
+                pltpu.VMEM((planes, 2, rows * rows // 2, chan), F32),
                 pltpu.VMEM((chips, per_owner, 2, rows * rows // 2, chan), F32),
                 pltpu.VMEM((flat, chan), F32),
                 pltpu.VMEM((flat, chan), F32),
@@ -632,6 +686,7 @@
                 pltpu.SemaphoreType.REGULAR,
                 pltpu.SemaphoreType.REGULAR,
                 dma((planes, 2)),
+                dma((planes, 2)),
                 dma((chips, per_owner, 2)),
                 dma((chips,)),
                 dma((chips,)),

time: 132 us -> 135 us (1.023)
  Pallas kernels: 131 us -> 133 us
    pallas_call x1, Pallas kernels: 131 us -> 133 us  [body(): pl.pallas_call(functools.partial(kernel, planes, chips, subs, heads), out...]
where the time goes in v5:
time: 135 us
  Pallas kernels  133 us (99%)
  local copies, waits for them, and re-layouts  1.69 us (1%)
    pallas_call x1, Pallas kernels, body(): pl.pallas_call(functools.partial(kernel, planes, chips, subs, heads), out...  133 us

profile of v5, /device:TPU:35, one launch (start us, length us, event | category | flops | bytes accessed | tf_op | source)
XLA Modules:
  0.0 134.8 jit_solution(17060936668725832439)
XLA Ops:
  0.0 133.1 %pair_update.1 = f32[12,48,128]{2,1,0:T(8,128)} custom-call(f32[12,48,128]{2,1,0:T(8,128)} %pair_ref.1, s32[384]{0:T(512)} %mask_ref.1, f32[1,128]{1,0:T(1,128)} %bitcast.9, bf16[512,128]{1,0:T(8,128)(2,1)} %bitcast.6, bf16[128,128]{1,0:T(8,128)(2,1)} %w_gate_ref.1, f32[1,128]{1,0:T(1,128)} %bitcast.10, bf16[128,128]{1,0:T(8,128)(2,1)} %w_tri_ref.1, ...), custom_call_target="tpu_custom_call" | custom-call | tf_op jit(solution)/shard_map/pair_update/pallas_call | solution.py:652
  133.1 1.7 %copy.13 = f32[12,48,128]{2,1,0:T(8,128)} copy(f32[12,48,128]{2,1,0:T(8,128)} %pair_update.1) | data formatting | bytes 589824

commit v6 on v4

--- a/solution.py
+++ b/solution.py
@@ -369,8 +369,6 @@
     by_distance = sorted(range(1, hops), key=lambda m: min(m, hops - m))
 
     def pass_bias(m):
-        if m:
-            bz_wait(lax.rem(z + STRIDE * m, planes))
         for n in range(len(near)):
 
             @pl.when(leaves(m, n))
@@ -386,8 +384,6 @@
     pl.semaphore_wait(mate_done, 1)
     for m in reversed(by_distance):
         bz_far_copy(m).start()
-    pl.semaphore_wait(plane_done, groups - 1)
-    pass_bias(0)
 
     def att_copy(source, target, sem):
         return pltpu.make_async_remote_copy(
@@ -402,12 +398,12 @@
     def att_across(d):
         return att_copy(g, {"col": lax.rem(x + d, chips)}, att_send.at[d])
 
-    def att_over(d):
-        return att_copy(lax.rem(x + d, chips) * subs + core, {"sub": mate}, att_pass.at[d])
+    def att_over(c):
+        return att_copy(c, {"sub": mate}, att_pass.at[c // subs])
 
     for d in sorted(range(1, chips), key=lambda d: -min(d, chips - d)):
         att_across(d).start()
-    att_over(0).start()
+    att_over(g).start()
 
     def att_weight(p):
         return weight_buf[pl.ds(p, chan, stride=4), :].astype(BF16)
@@ -456,21 +452,38 @@
     mate_copy(left_here.at[core], 1).wait_send()
     lax.fori_loop(0, planes, parts_sent, 0)
 
-    key_value(g)
-    waiting = list(by_distance)
-    for d in [0] + sorted(range(1, chips), key=lambda d: min(d, chips - d)):
-        if d:
-            c = lax.rem(x + d, chips) * subs + core
+    pl.semaphore_wait(plane_done, groups - 1)
+    pass_bias(0)
+
+    late = lax.rem(z + half, planes) // per_owner
+
+    def take_rows(k, carry):
+        c = lax.rem(late + k, groups)
+
+        @pl.when(c != g)
+        def _():
             att_wait(c)
-            att_over(d).start()
-            key_value(c)
-        c = lax.rem(x + d, chips) * subs + mate
-        att_wait(c)
+
+        @pl.when((c != g) & (lax.rem(c, subs) == core))
+        def _():
+            att_over(c).start()
+
         key_value(c)
-        if len(waiting) > 2:
-            for m in waiting[:2]:
-                pass_bias(m)
-            waiting = waiting[2:]
+        return carry
+
+    def take_bias(k, carry):
+        m = lax.rem(g + k + 2 * hops - z // STRIDE - hops // 2, hops)
+
+        @pl.when(m != 0)
+        def _():
+            bz_wait(lax.rem(z + STRIDE * m, planes))
+            pass_bias(m)
+
+        return carry
+
+    lax.fori_loop(1, groups, take_rows, 0)
+    lax.fori_loop(1, hops, take_bias, 0)
+    take_rows(groups, 0)
 
     lane_head = lax.broadcasted_iota(jnp.int32, (cols, chan), 1) // (chan // heads)
 
@@ -483,8 +496,7 @@
         return carry
 
     lax.fori_loop(0, rows, raw_scores, 0, unroll=2)
-    for m in waiting:
-        pass_bias(m)
+    take_bias(0, 0)
 
     for d in range(groups):
         c = lax.rem(g + d, groups)
@@ -553,7 +565,7 @@
     for d in range(chips):
         if d:
             att_across(d).wait_send()
-        att_over(d).wait_send()
+        att_over(d * subs + core).wait_send()
 
 
 def solution(mesh):

time: 132 us -> 136 us (1.030)
  the two profiles are of different devices: /device:TPU:35 before, /device:TPU:33 now
where the time goes in v6:
time: 136 us; the launch traced here: 135 us
  Pallas kernels  133 us (98%)
  local copies, waits for them, and re-layouts  1.69 us (1%)
    pallas_call x1, Pallas kernels, body(): pl.pallas_call(functools.partial(kernel, planes, chips, subs, heads), out...  133 us

profile of v6, /device:TPU:33, one launch (start us, length us, event | category | flops | bytes accessed | tf_op | source)
XLA Modules:
  0.0 134.7 jit_solution(17030294505714488961)
XLA Ops:
  0.0 133.0 %pair_update.1 = f32[12,48,128]{2,1,0:T(8,128)} custom-call(f32[12,48,128]{2,1,0:T(8,128)} %pair_ref.1, s32[384]{0:T(512)} %mask_ref.1, f32[1,128]{1,0:T(1,128)} %bitcast.9, bf16[512,128]{1,0:T(8,128)(2,1)} %bitcast.6, bf16[128,128]{1,0:T(8,128)(2,1)} %w_gate_ref.1, f32[1,128]{1,0:T(1,128)} %bitcast.10, bf16[128,128]{1,0:T(8,128)(2,1)} %w_tri_ref.1, ...), custom_call_target="tpu_custom_call" | custom-call | tf_op jit(solution)/shard_map/pair_update/pallas_call | solution.py:611
  133.0 1.7 %copy.13 = f32[12,48,128]{2,1,0:T(8,128)} copy(f32[12,48,128]{2,1,0:T(8,128)} %pair_update.1) | data formatting | bytes 589824

commit v7 on v6

--- a/solution.py
+++ b/solution.py
@@ -457,9 +457,7 @@
 
     late = lax.rem(z + half, planes) // per_owner
 
-    def take_rows(k, carry):
-        c = lax.rem(late + k, groups)
-
+    def take_rows(c):
         @pl.when(c != g)
         def _():
             att_wait(c)
@@ -469,7 +467,18 @@
             att_over(c).start()
 
         key_value(c)
-        return carry
+
+    def take_chip(of):
+        def body(d, carry):
+            c = lax.rem(late // subs + d, chips) * subs + of
+
+            @pl.when(c != late)
+            def _():
+                take_rows(c)
+
+            return carry
+
+        return body
 
     def take_bias(k, carry):
         m = lax.rem(g + k + 2 * hops - z // STRIDE - hops // 2, hops)
@@ -481,9 +490,10 @@
 
         return carry
 
-    lax.fori_loop(1, groups, take_rows, 0)
+    lax.fori_loop(1, chips + 1, take_chip(core), 0)
+    lax.fori_loop(1, chips + 1, take_chip(mate), 0)
     lax.fori_loop(1, hops, take_bias, 0)
-    take_rows(groups, 0)
+    take_rows(late)
 
     lane_head = lax.broadcasted_iota(jnp.int32, (cols, chan), 1) // (chan // heads)
 

time: 136 us -> 133 us (0.978); the launches traced: 135 us -> 130 us
  Pallas kernels: 133 us -> 128 us
    pallas_call x1, Pallas kernels: 133 us -> 128 us  [body(): pl.pallas_call(functools.partial(kernel, planes, chips, subs, heads), out...]
where the time goes in v7:
time: 133 us; the launch traced here: 130 us
  Pallas kernels  128 us (96%)
  local copies, waits for them, and re-layouts  1.69 us (1%)
    pallas_call x1, Pallas kernels, body(): pl.pallas_call(functools.partial(kernel, planes, chips, subs, heads), out...  128 us

profile of v7, /device:TPU:33, one launch (start us, length us, event | category | flops | bytes accessed | tf_op | source)
XLA Modules:
  0.0 130.2 jit_solution(3819877678761342011)
XLA Ops:
  0.0 128.4 %pair_update.1 = f32[12,48,128]{2,1,0:T(8,128)} custom-call(f32[12,48,128]{2,1,0:T(8,128)} %pair_ref.1, s32[384]{0:T(512)} %mask_ref.1, f32[1,128]{1,0:T(1,128)} %bitcast.9, bf16[512,128]{1,0:T(8,128)(2,1)} %bitcast.6, bf16[128,128]{1,0:T(8,128)(2,1)} %w_gate_ref.1, f32[1,128]{1,0:T(1,128)} %bitcast.10, bf16[128,128]{1,0:T(8,128)(2,1)} %w_tri_ref.1, ...), custom_call_target="tpu_custom_call" | custom-call | tf_op jit(solution)/shard_map/pair_update/pallas_call | solution.py:621
  128.5 1.7 %copy.13 = f32[12,48,128]{2,1,0:T(8,128)} copy(f32[12,48,128]{2,1,0:T(8,128)} %pair_update.1) | data formatting | bytes 589824

commit v8 on v7

--- a/solution.py
+++ b/solution.py
@@ -384,6 +384,8 @@
     pl.semaphore_wait(mate_done, 1)
     for m in reversed(by_distance):
         bz_far_copy(m).start()
+    pl.semaphore_wait(plane_done, groups - 1)
+    pass_bias(0)
 
     def att_copy(source, target, sem):
         return pltpu.make_async_remote_copy(
@@ -452,9 +454,6 @@
     mate_copy(left_here.at[core], 1).wait_send()
     lax.fori_loop(0, planes, parts_sent, 0)
 
-    pl.semaphore_wait(plane_done, groups - 1)
-    pass_bias(0)
-
     late = lax.rem(z + half, planes) // per_owner
 
     def take_rows(c):
@@ -505,7 +504,7 @@
         score_buf[i] = dot_nt(stack, key_buf[i])
         return carry
 
-    lax.fori_loop(0, rows, raw_scores, 0, unroll=2)
+    lax.fori_loop(0, rows, raw_scores, 0, unroll=4)
     take_bias(0, 0)
 
     for d in range(groups):
@@ -560,7 +559,7 @@
         gated_buf[here, :] = (attended * gate_buf[here, :]).astype(BF16)
         return carry
 
-    lax.fori_loop(0, rows, attend, 0, unroll=2)
+    lax.fori_loop(0, rows, attend, 0, unroll=4)
     out_ref[...] = (mid_buf[...] + dot(gated_buf[...], w_out_ref[...])).reshape(rows, cols, chan)
 
     for m in range(hops):

time: 133 us -> 130 us (0.977); the launches traced: 130 us -> 130 us
  no operation moved by 1% of the time
where the time goes in v8:
time: 130 us
  Pallas kernels  128 us (98%)
  local copies, waits for them, and re-layouts  1.69 us (1%)
    pallas_call x1, Pallas kernels, body(): pl.pallas_call(functools.partial(kernel, planes, chips, subs, heads), out...  128 us

profile of v8, /device:TPU:33, one launch (start us, length us, event | category | flops | bytes accessed | tf_op | source)
XLA Modules:
  0.0 129.8 jit_solution(18617367659320153)
XLA Ops:
  0.0 128.1 %pair_update.1 = f32[12,48,128]{2,1,0:T(8,128)} custom-call(f32[12,48,128]{2,1,0:T(8,128)} %pair_ref.1, s32[384]{0:T(512)} %mask_ref.1, f32[1,128]{1,0:T(1,128)} %bitcast.9, bf16[512,128]{1,0:T(8,128)(2,1)} %bitcast.6, bf16[128,128]{1,0:T(8,128)(2,1)} %w_gate_ref.1, f32[1,128]{1,0:T(1,128)} %bitcast.10, bf16[128,128]{1,0:T(8,128)(2,1)} %w_tri_ref.1, ...), custom_call_target="tpu_custom_call" | custom-call | tf_op jit(solution)/shard_map/pair_update/pallas_call | solution.py:620
  128.1 1.7 %copy.13 = f32[12,48,128]{2,1,0:T(8,128)} copy(f32[12,48,128]{2,1,0:T(8,128)} %pair_update.1) | data formatting | bytes 589824
